TPU v7x, 768 devices: a whole 4x8x12 slice. The times are simulated.
768 devices in a mesh: ta: 16 (over y, x_lo), sa: 48 (over x_hi, z, core).
Axes of the slice: x: 4 (x_hi: 2, x_lo: 2; x = x_hi * 2 + x_lo), y: 8, z: 12, core: 2. Of those that a mesh axis runs over, the one named last changes fastest.
Arguments:
- eigvecs: float32 [2, 32, 64, 3, 24576], P(None, 'ta', None, None, 'sa'), may hold values from -0.0234375 to 0.0234375
- solutions: float32 [2, 32, 3, 8, 4, 3, 24576], P(None, 'ta', None, None, None, None, 'sa'), may hold values from -15 to 15
- source_times: int32 [3], replicated, may hold values from 0 to 31, as said below
- spin_dilution: int32 [3, 8], replicated, may hold values from 0 to 3
Outputs:
- perambulator: float32 [2, 32, 6144], P(None, 'ta', 'sa')
- norms: float32 [3, 8], replicated
Inputs may be any that keep to these rules, and one draw needn't show every extreme that they name: `source_times`: some source lies at slice 0 and another at slice 32 - 1.
All inputs are finite; a program needn't handle non-finite values.
Results may differ from a plain program's by a relative error of at most 0.000084.
Values sent between devices are 32-bit elements; how exact they have to be, the bound alone decides.
A program may use at most 32 MiB of HBM per device.

v0:
```python
import functools

import jax
import jax.numpy as jnp
from jax import lax
from jax.sharding import Mesh
from jax.sharding import PartitionSpec as P

TA = ("ta_0", "ta_1")
SA = ("sa_0", "sa_1", "sa_2")
TA_SA = ("ta_0", "ta_1", "sa_0", "sa_1", "sa_2")


def over_axes(x, axes):
    return functools.reduce(lax.psum, axes, x)


def split_up(x, dim, count):
    lengths = x.shape
    tiles = x.reshape(*lengths[:dim], count, lengths[dim] // count, *lengths[dim + 1 :])
    return jnp.moveaxis(tiles, dim, 0)


def sent_and_summed(x, axis, dim):
    tiles = split_up(x, dim, lax.axis_size(axis))
    arrived = lax.all_to_all(tiles, axis, split_axis=0, concat_axis=0, tiled=True)
    return arrived.sum(axis=0)


def on_device(eigvecs, solutions, source_times, spin_dilution):
    time_rows = eigvecs.shape[1]
    eig_count = eigvecs.shape[2]
    site_count = eigvecs.shape[4]
    src_count = spin_dilution.shape[0]
    col_count = spin_dilution.shape[1]
    columns = src_count * col_count * 4
    inner_len = 3 * site_count
    all_cells = 12.0 * time_rows * lax.axis_size(TA) * site_count * lax.axis_size(SA)
    norm_parts = jnp.sum(solutions * solutions, axis=(0, 1, 4, 5, 6))
    eigen_rows = eigvecs.reshape(2, time_rows, eig_count, inner_len)
    solution_rows = solutions.reshape(2, time_rows, columns, inner_len)
    precise = lax.Precision.HIGHEST
    eig_real = eigen_rows[0]
    eig_conj = -eigen_rows[1]
    sol_real = solution_rows[0]
    sol_imag = solution_rows[1]
    first_prod = jnp.einsum(
        "tak,tnk->tan",
        eig_real + eig_conj,
        sol_real,
        precision=precise,
        preferred_element_type=jnp.float32,
    )
    second_prod = jnp.einsum(
        "tak,tnk->tan",
        eig_real,
        sol_imag - sol_real,
        precision=precise,
        preferred_element_type=jnp.float32,
    )
    third_prod = jnp.einsum(
        "tak,tnk->tan",
        eig_conj,
        sol_real + sol_imag,
        precision=precise,
        preferred_element_type=jnp.float32,
    )
    real_part = first_prod - third_prod
    imag_part = first_prod + second_prod
    slice_times = lax.axis_index(TA) * time_rows + jnp.arange(time_rows, dtype=jnp.int32)
    boundary = jnp.where(slice_times[:, None] < source_times[None, :], -1.0, 1.0).astype(
        jnp.float32
    )
    chirality = jnp.where(spin_dilution < 2, 1.0, -1.0).astype(jnp.float32)
    signs = jnp.broadcast_to(
        (boundary[:, :, None] * chirality[None])[:, :, :, None],
        (time_rows, src_count, col_count, 4),
    ).reshape(time_rows, columns)
    partial_value = (jnp.stack([real_part, imag_part]) * signs[None, :, None, :]).reshape(
        2, time_rows, eig_count * columns
    )
    norm_total = over_axes(norm_parts, TA_SA)
    perambulator = sent_and_summed(partial_value, SA, 2)
    return (perambulator, norm_total / all_cells)


def solution(mesh):
    finer = Mesh(mesh.devices.reshape(8, 2, 2, 12, 2), ("ta_0", "ta_1", "sa_0", "sa_1", "sa_2"))
    return jax.shard_map(
        on_device,
        mesh=finer,
        in_specs=(P(None, TA, None, None, SA), P(None, TA, None, None, None, None, SA), P(), P()),
        out_specs=(P(None, TA, SA), P()),
        check_vma=False,
    )
```

profile of v0, /device:TPU:1, one launch (start us, length us, event | category | flops | bytes accessed | tf_op | source)
XLA Modules:
  0.0 103.3 jit_solution(15895110604377335217)
XLA Ops:
  0.6 2.5 %slice_negate_fusion = (f32[1,2,64,3,512]{4,2,3,1,0:T(8,128)S(1)}, f32[1,2,64,3,512]{4,2,3,1,0:T(8,128)}) fusion(f32[2,2,64,3,512]{4,2,3,1,0:T(8,128)} %param.4), kind=kLoop, calls=%fused_computation.11 | loop fusion | flops 196608 | bytes 3145728 | tf_op jit(solution)/shard_map/neg | solution.py:44
  3.1 0.5 copy.21
  3.7 0.6 neg.7
  4.3 2.8 %copy.20 = f32[1,2,64,3,512]{4,3,2,1,0:T(4,128)} copy(f32[1,2,64,3,512]{4,2,3,1,0:T(8,128)} %get-tuple-element.5) | data formatting | bytes 1572864 | tf_op jit(solution)/shard_map/slice | solution.py:43
  7.1 2.5 %squeeze.10 = f32[2,64,1536]{2,1,0:T(8,128)} reshape(f32[1,2,64,3,512]{4,3,2,1,0:T(4,128)} %copy.20) | data formatting | bytes 1572864 | tf_op jit(solution)/shard_map/squeeze | solution.py:43
  9.6 1.6 %fusion.19 = (f32[1,2,3,8,4,3,512]{6,4,5,3,2,1,0:T(4,128)S(1)}, f32[1,2,3,8,4,3,512]{6,4,5,3,2,1,0:T(4,128)}) fusion(f32[2,2,3,8,4,3,512]{6,4,5,3,2,1,0:T(4,128)S(1)} %copy-done), kind=kLoop, calls=%fused_computation.19 | loop fusion | bytes 4718592 | tf_op jit(solution)/shard_map/slice | solution.py:46
  11.2 0.7 copy.23
  11.8 0.9 squeeze.12
  12.8 3.1 %copy.22 = f32[1,2,3,8,4,3,512]{6,5,4,3,2,1,0:T(4,128)} copy(f32[1,2,3,8,4,3,512]{6,4,5,3,2,1,0:T(4,128)} %get-tuple-element.3) | data formatting | bytes 2359296 | tf_op jit(solution)/shard_map/slice | solution.py:45
  15.9 2.0 %squeeze.11 = f32[2,96,1536]{2,1,0:T(8,128)S(1)} reshape(f32[1,2,3,8,4,3,512]{6,5,4,3,2,1,0:T(4,128)} %copy.22) | data formatting | bytes 2359296 | tf_op jit(solution)/shard_map/squeeze | solution.py:45
  17.9 2.5 %fusion.16 = f32[2,64,96]{2,1,0:T(8,128)S(1)} fusion(f32[2,96,1536]{2,1,0:T(8,128)S(1)} %squeeze.11, f32[2,64,1536]{2,1,0:T(8,128)} %squeeze.10, f32[2,64,1536]{2,1,0:T(8,128)S(1)} %neg.7), kind=kOutput, calls=%fused_computation.9 | convolution fusion | flops 226689024 | bytes 2801664 | tf_op jit(solution)/shard_map/tak,tnk->tan/dot_general | solution.py:47
  20.5 1.5 %fusion.13 = f32[2,64,96]{2,1,0:T(8,128)S(1)} fusion(f32[2,64,96]{2,1,0:T(8,128)S(1)} %fusion.16, f32[2,64,1536]{2,1,0:T(8,128)S(1)} %copy-done.1, f32[2,96,1536]{2,1,0:T(8,128)S(1)} %squeeze.12, f32[2,96,1536]{2,1,0:T(8,128)S(1)} %squeeze.11), kind=kOutput, calls=%fused_computation.8 | convolution fusion | flops 226799616 | bytes 3244032 | tf_op jit(solution)/shard_map/tak,tnk->tan/dot_general | solution.py:54
  22.0 1.4 %fusion.7 = f32[2,64,96]{2,1,0:T(8,128)S(1)} fusion(f32[2,64,96]{2,1,0:T(8,128)S(1)} %fusion.16, f32[2,64,1536]{2,1,0:T(8,128)S(1)} %neg.7, f32[2,96,1536]{2,1,0:T(8,128)S(1)} %squeeze.11, f32[2,96,1536]{2,1,0:T(8,128)S(1)} %squeeze.12), kind=kOutput, calls=%fused_computation.6 | convolution fusion | flops 226799616 | bytes 3244032 | tf_op jit(solution)/shard_map/tak,tnk->tan/dot_general | solution.py:61
  23.7 0.1 mul.46
  24.2 0.7 fusion.18
  24.9 19.4 %all-to-all-start = ((f32[48,2,2,128]{3,2,1,0:T(2,128)}), f32[48,2,2,128]{3,2,1,0:T(2,128)S(1)}, u32[]{:S(2)}, u32[]{:S(2)}) async-start(f32[48,2,2,128]{3,2,1,0:T(2,128)} %fusion.18), calls=%async_computation | async-start | bytes 196608 | tf_op jit(solution)/shard_map/all_to_all | solution.py:26
  44.3 2.3 %multiply_reduce_fusion = f32[3,8]{1,0:T(4,128)S(1)} fusion(f32[2,2,3,8,4,3,512]{6,4,5,3,2,1,0:T(4,128)} %param.5), kind=kLoop, calls=%fused_computation | loop fusion | flops 1179624 | bytes 2359392 | tf_op jit(solution)/shard_map/reduce_sum | solution.py:39
  46.6 14.7 %psum.35 = f32[3,8]{1,0:T(4,128)S(1)} all-reduce(f32[3,8]{1,0:T(4,128)S(1)} %multiply_reduce_fusion), channel_id=1, replica_groups=mesh['ta_0'=8,'ta_1'=2,'sa_0'=2,'sa_1'=12,'sa_2'=2] {'ta_0'}, use_global_device_ids=true, to_apply=%region_2.3 | all-reduce | flops 24 | bytes 192 | tf_op jit(solution)/shard_map/psum | solution.py:15
  61.3 3.8 %psum.36 = f32[3,8]{1,0:T(4,128)S(1)} all-reduce(f32[3,8]{1,0:T(4,128)S(1)} %psum.35), channel_id=1, replica_groups=mesh['ta_0'=8,'ta_1'=2,'sa_0'=2,'sa_1'=12,'sa_2'=2] {'ta_1'}, use_global_device_ids=true, to_apply=%region_3.4 | all-reduce | flops 24 | bytes 192 | tf_op jit(solution)/shard_map/psum | solution.py:15
  65.1 5.3 %psum.37 = f32[3,8]{1,0:T(4,128)S(1)} all-reduce(f32[3,8]{1,0:T(4,128)S(1)} %psum.36), channel_id=1, replica_groups=mesh['ta_0'=8,'ta_1'=2,'sa_0'=2,'sa_1'=12,'sa_2'=2] {'sa_0'}, use_global_device_ids=true, to_apply=%region_4.5 | all-reduce | flops 24 | bytes 192 | tf_op jit(solution)/shard_map/psum | solution.py:15
  70.4 18.1 %psum.38 = f32[3,8]{1,0:T(4,128)S(1)} all-reduce(f32[3,8]{1,0:T(4,128)S(1)} %psum.37), channel_id=1, replica_groups=mesh['ta_0'=8,'ta_1'=2,'sa_0'=2,'sa_1'=12,'sa_2'=2] {'sa_1'}, use_global_device_ids=true, to_apply=%region_5.6 | all-reduce | flops 24 | bytes 192 | tf_op jit(solution)/shard_map/psum | solution.py:15
  88.4 13.6 %psum.39 = f32[3,8]{1,0:T(4,128)S(1)} all-reduce(f32[3,8]{1,0:T(4,128)S(1)} %psum.38), channel_id=1, replica_groups=mesh['ta_0'=8,'ta_1'=2,'sa_0'=2,'sa_1'=12,'sa_2'=2] {'sa_2'}, use_global_device_ids=true, to_apply=%region_6.7 | all-reduce | flops 24 | bytes 192 | tf_op jit(solution)/shard_map/psum | solution.py:15
  102.1 0.6 broadcast_multiply_fusion.1
  102.6 0.6 reduce_sum.18
  (21 shorter events, 0.6 us)
Async XLA Ops:
  4.3 5.3 %copy-start = (f32[2,2,3,8,4,3,512]{6,4,5,3,2,1,0:T(4,128)S(1)}, f32[2,2,3,8,4,3,512]{6,4,5,3,2,1,0:T(4,128)}, u32[]{:S(2)}) copy-start(f32[2,2,3,8,4,3,512]{6,4,5,3,2,1,0:T(4,128)} %param.5) | copy-start | bytes 7077892
  17.9 2.6 %copy-start.1 = (f32[2,64,1536]{2,1,0:T(8,128)S(1)}, f32[2,64,1536]{2,1,0:T(8,128)}, u32[]{:S(2)}) copy-start(f32[2,64,1536]{2,1,0:T(8,128)} %squeeze.10) | copy-start | bytes 2359300
  22.0 1.5 %copy-start.2 = (s32[3,8]{1,0:T(4,128)S(1)}, s32[3,8]{1,0:T(4,128)}, u32[]{:S(2)}) copy-start(s32[3,8]{1,0:T(4,128)} %param.7) | copy-start | bytes 292
  22.0 1.5 %copy-start.3 = (s32[3]{0:T(128)S(1)}, s32[3]{0:T(128)}, u32[]{:S(2)}) copy-start(s32[3]{0:T(128)} %param.6) | copy-start | bytes 40
  24.9 77.8 %all-to-all-start = ((f32[48,2,2,128]{3,2,1,0:T(2,128)}), f32[48,2,2,128]{3,2,1,0:T(2,128)S(1)}, u32[]{:S(2)}, u32[]{:S(2)}) async-start(f32[48,2,2,128]{3,2,1,0:T(2,128)} %fusion.18), calls=%async_computation | async-start | bytes 196608 | tf_op jit(solution)/shard_map/all_to_all | solution.py:26
where the time goes:
time: 104 us; the launch traced here: 103 us
  blocking collectives  55.5 us (53%)
  starting transfers between devices  19.4 us (19%)
  local copies, waits for them, and re-layouts  15.3 us (15%)
  other arithmetic  6.81 us (7%)
  matrix products  5.45 us (5%)
    psum x5, blocking collectives, over_axes(): return functools.reduce(lax.psum, axes, x)  55.5 us
    all_to_all x1, starting transfers between devices, sent_and_summed(): lax.all_to_all(tiles, axis, split_axis=0, concat_axis=0, tiled=True)  19.4 us
    slice x1, local copies, waits for them, and re-layouts, on_device(): sol_real = solution_rows[0]  3.1 us
    slice x1, local copies, waits for them, and re-layouts, on_device(): eig_real = eigen_rows[0]  2.82 us
    dot_general x1, matrix products, on_device(): jnp.einsum('tak,tnk->tan', eig_real + eig_conj, sol_real, precision=preci...  2.54 us
    neg x1, other arithmetic, on_device(): eig_conj = -eigen_rows[1]  2.5 us
    squeeze x1, local copies, waits for them, and re-layouts, on_device(): eig_real = eigen_rows[0]  2.48 us
    reduce_sum x1, other arithmetic, on_device(): norm_parts = jnp.sum(solutions * solutions, axis=(0, 1, 4, 5, 6))  2.26 us
  transfers between devices with their start and end apart: 1, of which 0 were waited for; matrix products, arithmetic and copies ran while one was open for 3% of the time, Pallas kernels for 0%

commit v1 on v0

v1 whole, which is shorter than its diff:
```python
import jax
import jax.numpy as jnp
from jax import lax
from jax.experimental import pallas as pl
from jax.experimental.pallas import tpu as pltpu
from jax.sharding import Mesh
from jax.sharding import PartitionSpec as P

F32 = jnp.float32
BF16 = jnp.bfloat16
MESH = pl.DeviceIdType.MESH
NY, NXL, NXH, NZ, NC = 8, 2, 2, 12, 2
TA = ("y", "xl")
SA = ("xh", "z", "core")
NEAR = NZ * NC
PLANE = NXH * NY * NXL


def split(x):
    high = x.astype(BF16)
    low = (x - high.astype(F32)).astype(BF16)
    return high, low


def dot_rows(a, b):
    return lax.dot_general(a, b, (((1,), (1,)), ((), ())), preferred_element_type=F32)


def kernel(times_ref, spin_ref, eig_hbm, sol_hbm, out_ref, norm_ref,
           eig, sol, tmp, send, recv, half, other, nsend1, nrecv1, nsend2, nrecv2,
           load_sem, ssem, rsem):
    y, xl, xh = lax.axis_index("y"), lax.axis_index("xl"), lax.axis_index("xh")
    z, core = lax.axis_index("z"), lax.axis_index("core")
    near_id = z * NC + core
    plane_id = (xh * NY + y) * NXL + xl

    def loads(t):
        copies = []
        for p in range(2):
            copies.append(pltpu.make_async_copy(eig_hbm.at[p, t], eig.at[p, t], load_sem.at[t]))
            for c in range(3):
                for j in range(4):
                    copies.append(pltpu.make_async_copy(
                        sol_hbm.at[p, t, :, c, :, pl.ds(128 * j, 128)],
                        sol.at[p, t, c, j], load_sem.at[t]))
        return copies

    for t in range(2):
        for copy in loads(t):
            copy.start()

    def near_peer(i):
        d = lax.rem(near_id + i, NEAR)
        return {"z": d // NC, "core": lax.rem(d, NC)}

    def plane_peer(i):
        d = lax.rem(plane_id + i, PLANE)
        return {"xh": d // (NY * NXL), "y": lax.rem(d // NXL, NY), "xl": lax.rem(d, NXL)}

    barrier = pltpu.get_barrier_semaphore()

    @pl.loop(1, NEAR)
    def _(i):
        pl.semaphore_signal(barrier, inc=1, device_id=near_peer(i), device_id_type=MESH)

    @pl.loop(1, PLANE)
    def _(i):
        pl.semaphore_signal(barrier, inc=1, device_id=plane_peer(i), device_id_type=MESH)

    lane = lax.broadcasted_iota(jnp.int32, (1, 128), 1)
    signs = []
    for t in range(2):
        now = (y * NXL + xl) * 2 + t
        sign = jnp.ones((1, 128), F32)
        for s in range(3):
            edge = jnp.where(now < times_ref[s], F32(-1), F32(1))
            for k in range(8):
                chir = jnp.where(spin_ref[s, k] < 2, F32(1), F32(-1))
                sign = jnp.where(lane // 4 == s * 8 + k, edge * chir, sign)
        signs.append(sign)

    squares = jnp.zeros((96, 128), F32)
    lane16 = lax.broadcasted_iota(jnp.int32, (16, 128), 1)
    for t in range(2):
        for copy in loads(t):
            copy.wait()
        prod = jnp.zeros((128, 256), F32)
        for c in range(3):
            e = jnp.concatenate([eig[0, t, c], eig[1, t, c]], axis=0)
            rows = []
            for p in range(2):
                pieces = []
                for j in range(4):
                    piece = sol[p, t, c, j].reshape(96, 128)
                    squares = squares + piece * piece
                    pieces.append(piece)
                rows.append(jnp.concatenate(pieces, axis=1))
                rows.append(jnp.zeros((32, 512), F32))
            s = jnp.concatenate(rows, axis=0)
            eh, el = split(e)
            sh, sl = split(s)
            prod = prod + (dot_rows(eh, sh) + (dot_rows(eh, sl) + dot_rows(el, sh)))
        real = (prod[:64, :128] + prod[64:, 128:]) * signs[t]
        imag = (prod[:64, 128:] - prod[64:, :128]) * signs[t]
        for p, part in enumerate((real, imag)):
            tmp[...] = part
            a0 = tmp[pl.ds(0, 16, stride=4), :]
            r1 = pltpu.roll(tmp[pl.ds(1, 16, stride=4), :], 96, 1)
            r2 = pltpu.roll(tmp[pl.ds(2, 16, stride=4), :], 64, 1)
            r3 = pltpu.roll(tmp[pl.ds(3, 16, stride=4), :], 32, 1)
            blocks = (jnp.where(lane16 < 96, a0, r1), jnp.where(lane16 < 64, r1, r2),
                      jnp.where(lane16 < 32, r2, r3))
            for r, block in enumerate(blocks):
                for h in range(2):
                    send[pl.ds(r * 8 + h * 4 + p * 2 + t, 8, stride=24), :] = block[8 * h:8 * h + 8]

    total = jnp.sum(squares, axis=1, keepdims=True)
    row = lax.broadcasted_iota(jnp.int32, (96, 128), 0)
    col = lax.broadcasted_iota(jnp.int32, (96, 128), 1)
    nsend1[...] = jnp.sum(jnp.where(row // 4 == col, total, F32(0)), axis=0, keepdims=True)

    pl.semaphore_wait(barrier, NEAR - 1 + PLANE - 1)

    def near_norm(i):
        return pltpu.make_async_remote_copy(
            src_ref=nsend1, dst_ref=nrecv1.at[near_id], send_sem=ssem.at[0], recv_sem=rsem.at[0],
            device_id=near_peer(i), device_id_type=MESH)

    def near_block(i):
        peer = lax.rem(near_id + i, NEAR)
        return pltpu.make_async_remote_copy(
            src_ref=send.at[pl.ds(pl.multiple_of(peer * 8, 8), 8)], dst_ref=recv.at[near_id],
            send_sem=ssem.at[1], recv_sem=rsem.at[1],
            device_id=near_peer(i), device_id_type=MESH)

    def plane_norm(i):
        return pltpu.make_async_remote_copy(
            src_ref=nsend2, dst_ref=nrecv2.at[plane_id], send_sem=ssem.at[2], recv_sem=rsem.at[2],
            device_id=plane_peer(i), device_id_type=MESH)

    def middle_out(i, n):
        m = n // 2
        return m + jnp.where(lax.rem(i, 2) == 0, -(i // 2), (i + 1) // 2)

    @pl.loop(0, NEAR - 1)
    def _(i):
        near_norm(middle_out(i, NEAR)).start()

    @pl.loop(0, NEAR - 1)
    def _(i):
        near_block(middle_out(i, NEAR)).start()

    nrecv1[near_id] = nsend1[...]
    recv[near_id] = send[pl.ds(pl.multiple_of(near_id * 8, 8), 8), :]

    def arrived(buf, count, sem):
        pltpu.make_async_copy(buf.at[pl.ds(0, count)], buf.at[pl.ds(0, count)], sem).wait()

    arrived(nrecv1, NEAR - 1, rsem.at[0])
    nsend2[...] = jnp.sum(nrecv1[...], axis=0)

    @pl.loop(1, PLANE)
    def _(i):
        plane_norm(i).start()

    arrived(recv, NEAR - 1, rsem.at[1])
    block = jnp.sum(recv[...], axis=0)
    half[0] = block[:4]
    half[1] = block[4:]
    cross = pltpu.make_async_remote_copy(
        src_ref=half.at[1 - xh], dst_ref=other, send_sem=ssem.at[3], recv_sem=rsem.at[3],
        device_id={"xh": 1 - xh}, device_id_type=MESH)
    cross.start()
    nrecv2[plane_id] = nsend2[...]
    cross.wait()
    mine = half[xh] + other[...]
    out_ref[0] = mine[:2]
    out_ref[1] = mine[2:]

    arrived(nrecv2, PLANE - 1, rsem.at[2])
    norm = jnp.sum(nrecv2[...], axis=0) / F32(9437184.0)
    for s in range(3):
        norm_ref[s:s + 1, :] = pltpu.roll(norm, (128 - 8 * s) % 128, 1)[:, :8]

    arrived(nrecv1, NEAR - 1, ssem.at[0])
    arrived(recv, NEAR - 1, ssem.at[1])
    arrived(nrecv2, PLANE - 1, ssem.at[2])


def on_device(eigvecs, solutions, source_times, spin_dilution):
    eig = jnp.transpose(eigvecs, (0, 1, 3, 2, 4))
    sol = jnp.transpose(solutions, (0, 1, 2, 3, 5, 4, 6)).reshape(2, 2, 24, 3, 4, 512)
    vmem = pl.BlockSpec(memory_space=pltpu.VMEM)
    smem = pl.BlockSpec(memory_space=pltpu.SMEM)
    hbm = pl.BlockSpec(memory_space=pl.ANY)
    return pl.pallas_call(
        kernel,
        out_shape=(jax.ShapeDtypeStruct((2, 2, 128), F32), jax.ShapeDtypeStruct((3, 8), F32)),
        in_specs=[smem, smem, hbm, hbm],
        out_specs=(vmem, vmem),
        scratch_shapes=[
            pltpu.VMEM((2, 2, 3, 64, 512), F32),
            pltpu.VMEM((2, 2, 3, 4, 24, 4, 128), F32),
            pltpu.VMEM((64, 128), F32),
            pltpu.VMEM((NEAR * 8, 128), F32),
            pltpu.VMEM((NEAR, 8, 128), F32),
            pltpu.VMEM((2, 4, 128), F32),
            pltpu.VMEM((4, 128), F32),
            pltpu.VMEM((1, 128), F32),
            pltpu.VMEM((NEAR, 1, 128), F32),
            pltpu.VMEM((1, 128), F32),
            pltpu.VMEM((PLANE, 1, 128), F32),
            pltpu.SemaphoreType.DMA((2,)),
            pltpu.SemaphoreType.DMA((4,)),
            pltpu.SemaphoreType.DMA((4,)),
        ],
        compiler_params=pltpu.CompilerParams(collective_id=0, has_side_effects=True),
        name="perambulator",
    )(source_times, spin_dilution, eig, sol)


def solution(mesh):
    finer = Mesh(mesh.devices.reshape(NY, NXL, NXH, NZ, NC), TA + SA)
    return jax.shard_map(
        on_device,
        mesh=finer,
        in_specs=(P(None, TA, None, None, SA), P(None, TA, None, None, None, None, SA), P(), P()),
        out_specs=(P(None, TA, SA), P()),
        check_vma=False,
    )
```

time: 104 us -> 36.5 us (0.35)
  blocking collectives: 55.5 us -> 0 us
  Pallas kernels: 0 us -> 33.2 us
  starting transfers between devices: 19.4 us -> 0 us
  local copies, waits for them, and re-layouts: 15.3 us -> 2.48 us
  other arithmetic: 6.81 us -> 0 us
  matrix products: 5.45 us -> 0 us
    psum x5 -> x0, blocking collectives: 55.5 us -> none  [over_axes(): return functools.reduce(lax.psum, axes, x)]
    pallas_call x0 -> x1, Pallas kernels: none -> 33.2 us  [on_device(): pl.pallas_call(kernel, out_shape=(jax.ShapeDtypeStruct((2, 2, 128), F32),...]
    all_to_all x1 -> x0, starting transfers between devices: 19.4 us -> none  [sent_and_summed(): lax.all_to_all(tiles, axis, split_axis=0, concat_axis=0, tiled=True)]
    slice x4 -> x0, local copies, waits for them, and re-layouts: 8.16 us -> none  [the longest x1 3.1 us: on_device(): sol_real = solution_rows[0]]
    dot_general x3 -> x0, matrix products: 5.45 us -> none  [the longest x1 2.54 us: on_device(): jnp.einsum('tak,tnk->tan', eig_real + eig_conj, sol_real, precision=preci...]
    squeeze x3 -> x0, local copies, waits for them, and re-layouts: 5.44 us -> none  [the longest x1 2.48 us: on_device(): eig_real = eigen_rows[0]]
    reduce_sum x2 -> x0, other arithmetic: 2.9 us -> none  [the longest x1 2.26 us: on_device(): norm_parts = jnp.sum(solutions * solutions, axis=(0, 1, 4, 5, 6))]
    neg x1 -> x0, other arithmetic: 2.5 us -> none  [on_device(): eig_conj = -eigen_rows[1]]
  transfers between devices with their start and end apart: 1 -> 0, of which waited for: 0 -> 0; matrix products, arithmetic and copies ran while one was open for 3% -> 0% of each run, Pallas kernels for 0% -> 0%
where the time goes in v1:
time: 36.5 us; the launch traced here: 36.3 us
  Pallas kernels  33.2 us (91%)
  local copies, waits for them, and re-layouts  2.48 us (7%)
  between operations  0.64 us (2%)
    pallas_call x1, Pallas kernels, on_device(): pl.pallas_call(kernel, out_shape=(jax.ShapeDtypeStruct((2, 2, 128), F32),...  33.2 us
    unnamed x2, local copies, waits for them, and re-layouts  2.48 us

profile of v1, /device:TPU:1, one launch (start us, length us, event | category | flops | bytes accessed | tf_op | source)
XLA Modules:
  0.0 36.3 jit_solution(12103476480148521086)
XLA Ops:
  0.6 33.2 %perambulator.1 = (f32[2,2,128]{2,1,0:T(2,128)}, f32[3,8]{1,0:T(4,128)}) custom-call(s32[3]{0:T(128)} %times_ref.1, s32[3,8]{1,0:T(4,128)} %spin_ref.1, f32[2,2,3,64,512]{4,3,2,1,0:T(8,128)} %bitcast.5, f32[2,2,24,3,4,512]{5,4,3,2,1,0:T(4,128)} %bitcast.4), custom_call_target="tpu_custom_call" | custom-call | tf_op jit(solution)/shard_map/perambulator/pallas_call | solution.py:196
  33.8 1.2 %copy.8 = f32[2,2,128]{2,1,0:T(2,128)} copy(f32[2,2,128]{2,1,0:T(2,128)} %get-tuple-element.4) | data formatting | bytes 4096
  35.1 1.2 %copy.9 = f32[3,8]{1,0:T(4,128)} copy(f32[3,8]{1,0:T(4,128)} %get-tuple-element.5) | data formatting | bytes 192

commit v2 on v1

v2 whole, which is shorter than its diff:
```python
import jax
import jax.numpy as jnp
from jax import lax
from jax.experimental import pallas as pl
from jax.experimental.pallas import tpu as pltpu
from jax.sharding import Mesh
from jax.sharding import PartitionSpec as P

F32 = jnp.float32
BF16 = jnp.bfloat16
MESH = pl.DeviceIdType.MESH
NY, NXL, NXH, NZ, NC = 8, 2, 2, 12, 2
TA = ("y", "xl")
SA = ("xh", "z", "core")
COLUMN = NZ * NC
PLANE = NXH * NY * NXL


def split(x):
    high = x.astype(BF16)
    low = (x - high.astype(F32)).astype(BF16)
    return high, low


def dot_rows(a, b):
    return lax.dot_general(a, b, (((1,), (1,)), ((), ())), preferred_element_type=F32)


def kernel(times_ref, spin_ref, eig_hbm, sol_hbm, out_ref, norm_ref,
           eig, sol, tmp, send, recv, half, other, row, rows1, total, rows2, final,
           sol_sem, eig_sem, ssem, rsem, ready):
    y, xl, xh = lax.axis_index("y"), lax.axis_index("xl"), lax.axis_index("xh")
    z, core = lax.axis_index("z"), lax.axis_index("core")
    me = z * NC + 1 - core
    plane_me = (xh * NY + y) * NXL + xl
    is_root = me == 0

    def sol_loads(p, t):
        return [pltpu.make_async_copy(sol_hbm.at[p, t, :, c, :, pl.ds(128 * j, 128)],
                                      sol.at[p, t, c, j], sol_sem.at[p, t])
                for c in range(3) for j in range(4)]

    def eig_loads(t):
        return [pltpu.make_async_copy(eig_hbm.at[p, t], eig.at[p, t], eig_sem.at[t])
                for p in range(2)]

    for t in range(2):
        for p in range(2):
            for copy in sol_loads(p, t):
                copy.start()
    for t in range(2):
        for copy in eig_loads(t):
            copy.start()

    def column(o):
        return {"z": o // NC, "core": 1 - lax.rem(o, NC)}

    def plane(i):
        d = lax.rem(plane_me + i, PLANE)
        return {"xh": d // (NY * NXL), "y": lax.rem(d // NXL, NY), "xl": lax.rem(d, NXL)}

    barrier = pltpu.get_barrier_semaphore()

    @pl.loop(me + 1, COLUMN)
    def _(o):
        pl.semaphore_signal(barrier, inc=1, device_id=column(o), device_id_type=MESH)

    pl.semaphore_signal(barrier, inc=1, device_id={"xh": 1 - xh}, device_id_type=MESH)

    @pl.when(is_root)
    def _():
        @pl.loop(1, PLANE)
        def _(i):
            pl.semaphore_signal(barrier, inc=1, device_id=plane(i), device_id_type=MESH)

    squares = jnp.zeros((96, 128), F32)
    for t in range(2):
        for p in range(2):
            for copy in sol_loads(p, t):
                copy.wait()
            for c in range(3):
                for j in range(4):
                    piece = sol[p, t, c, j].reshape(96, 128)
                    squares = squares + piece * piece
        if t == 0:
            pl.semaphore_wait(barrier, me + 1 + jnp.where(is_root, PLANE - 1, 0))

            @pl.loop(0, me)
            def _(o):
                pl.semaphore_signal(ready, inc=1, device_id=column(o), device_id_type=MESH)

    sums = jnp.sum(squares, axis=1, keepdims=True)
    line = lax.broadcasted_iota(jnp.int32, (96, 128), 0)
    spot = lax.broadcasted_iota(jnp.int32, (96, 128), 1)
    row[...] = jnp.sum(jnp.where(line // 4 == spot, sums, F32(0)), axis=0, keepdims=True)

    up = pltpu.make_async_remote_copy(
        src_ref=row, dst_ref=rows1.at[me], send_sem=ssem.at[0], recv_sem=rsem.at[0],
        device_id={"z": 0, "core": 1}, device_id_type=MESH)

    @pl.when(jnp.logical_not(is_root))
    def _():
        up.start()

    lane = lax.broadcasted_iota(jnp.int32, (1, 128), 1)
    lane16 = lax.broadcasted_iota(jnp.int32, (16, 128), 1)
    for t in range(2):
        now = (y * NXL + xl) * 2 + t
        sign = jnp.ones((1, 128), F32)
        for s in range(3):
            edge = jnp.where(now < times_ref[s], F32(-1), F32(1))
            for k in range(8):
                chir = jnp.where(spin_ref[s, k] < 2, F32(1), F32(-1))
                sign = jnp.where(lane // 4 == s * 8 + k, edge * chir, sign)
        for copy in eig_loads(t):
            copy.wait()
        prod = jnp.zeros((128, 256), F32)
        for c in range(3):
            e = jnp.concatenate([eig[0, t, c], eig[1, t, c]], axis=0)
            parts = []
            for p in range(2):
                parts.append(jnp.concatenate(
                    [sol[p, t, c, j].reshape(96, 128) for j in range(4)], axis=1))
                parts.append(jnp.zeros((32, 512), F32))
            s = jnp.concatenate(parts, axis=0)
            eh, el = split(e)
            sh, sl = split(s)
            prod = prod + (dot_rows(eh, sh) + (dot_rows(eh, sl) + dot_rows(el, sh)))
        real = (prod[:64, :128] + prod[64:, 128:]) * sign
        imag = (prod[:64, 128:] - prod[64:, :128]) * sign
        for p, part in enumerate((real, imag)):
            tmp[...] = part
            a0 = tmp[pl.ds(0, 16, stride=4), :]
            r1 = pltpu.roll(tmp[pl.ds(1, 16, stride=4), :], 96, 1)
            r2 = pltpu.roll(tmp[pl.ds(2, 16, stride=4), :], 64, 1)
            r3 = pltpu.roll(tmp[pl.ds(3, 16, stride=4), :], 32, 1)
            blocks = (jnp.where(lane16 < 96, a0, r1), jnp.where(lane16 < 64, r1, r2),
                      jnp.where(lane16 < 32, r2, r3))
            for r, block in enumerate(blocks):
                for h in range(2):
                    send[pl.ds(r * 8 + h * 4 + p * 2 + t, 8, stride=24), :] = block[8 * h:8 * h + 8]

    def send_block(o):
        peer = column(o)
        place = pl.multiple_of((peer["z"] * NC + peer["core"]) * 8, 8)
        pltpu.make_async_remote_copy(
            src_ref=send.at[pl.ds(place, 8)], dst_ref=recv.at[me],
            send_sem=ssem.at[1], recv_sem=rsem.at[1],
            device_id=peer, device_id_type=MESH).start()

    @pl.loop(0, me)
    def _(o):
        send_block(o)

    @pl.when(me < COLUMN - 1)
    def _():
        pl.semaphore_wait(ready, COLUMN - 1 - me)

    @pl.loop(me + 1, COLUMN)
    def _(o):
        send_block(o)

    recv[me] = send[pl.ds(pl.multiple_of((z * NC + core) * 8, 8), 8), :]

    def arrived(buf, count, sem):
        pltpu.make_async_copy(buf.at[pl.ds(0, count)], buf.at[pl.ds(0, count)], sem).wait()

    @pl.when(is_root)
    def _():
        rows1[0] = row[...]
        arrived(rows1, COLUMN - 1, rsem.at[0])
        total[...] = jnp.sum(rows1[...], axis=0)

        @pl.loop(1, PLANE)
        def _(i):
            pltpu.make_async_remote_copy(
                src_ref=total, dst_ref=rows2.at[plane_me], send_sem=ssem.at[2], recv_sem=rsem.at[2],
                device_id=plane(i), device_id_type=MESH).start()

        rows2[plane_me] = total[...]

    arrived(recv, COLUMN - 1, rsem.at[1])
    block = jnp.sum(recv[...], axis=0)
    half[0] = block[:4]
    half[1] = block[4:]
    cross = pltpu.make_async_remote_copy(
        src_ref=half.at[1 - xh], dst_ref=other, send_sem=ssem.at[3], recv_sem=rsem.at[3],
        device_id={"xh": 1 - xh}, device_id_type=MESH)
    cross.start()
    cross.wait()
    mine = half[xh] + other[...]
    out_ref[0] = mine[:2]
    out_ref[1] = mine[2:]

    def down(o):
        return pltpu.make_async_remote_copy(
            src_ref=final, dst_ref=final, send_sem=ssem.at[4], recv_sem=rsem.at[4],
            device_id=column(o), device_id_type=MESH)

    @pl.when(is_root)
    def _():
        arrived(rows2, PLANE - 1, rsem.at[2])
        final[...] = jnp.sum(rows2[...], axis=0)

        @pl.loop(1, COLUMN)
        def _(o):
            down(o).start()

    @pl.when(jnp.logical_not(is_root))
    def _():
        down(0).wait_recv()

    norm = final[...] / F32(9437184.0)
    for s in range(3):
        norm_ref[s:s + 1, :] = pltpu.roll(norm, (128 - 8 * s) % 128, 1)[:, :8]

    arrived(recv, COLUMN - 1, ssem.at[1])

    @pl.when(is_root)
    def _():
        arrived(rows2, PLANE - 1, ssem.at[2])
        arrived(rows1, COLUMN - 1, ssem.at[4])

    @pl.when(jnp.logical_not(is_root))
    def _():
        up.wait_send()


def finish(block_ref, norm_ref, block_out, norm_out, sem):
    copies = [pltpu.make_async_copy(block_ref, block_out, sem.at[0]),
              pltpu.make_async_copy(norm_ref, norm_out, sem.at[1])]
    for copy in copies:
        copy.start()
    for copy in copies:
        copy.wait()


def on_device(eigvecs, solutions, source_times, spin_dilution):
    eig = jnp.transpose(eigvecs, (0, 1, 3, 2, 4))
    sol = jnp.transpose(solutions, (0, 1, 2, 3, 5, 4, 6)).reshape(2, 2, 24, 3, 4, 512)
    vmem = pl.BlockSpec(memory_space=pltpu.VMEM)
    smem = pl.BlockSpec(memory_space=pltpu.SMEM)
    hbm = pl.BlockSpec(memory_space=pl.ANY)
    results = (jax.ShapeDtypeStruct((2, 2, 128), F32), jax.ShapeDtypeStruct((3, 8), F32))
    block, norm = pl.pallas_call(
        kernel,
        out_shape=(pltpu.VMEM((2, 2, 128), F32), pltpu.VMEM((3, 8), F32)),
        in_specs=[smem, smem, hbm, hbm],
        out_specs=(vmem, vmem),
        scratch_shapes=[
            pltpu.VMEM((2, 2, 3, 64, 512), F32),
            pltpu.VMEM((2, 2, 3, 4, 24, 4, 128), F32),
            pltpu.VMEM((64, 128), F32),
            pltpu.VMEM((COLUMN * 8, 128), F32),
            pltpu.VMEM((COLUMN, 8, 128), F32),
            pltpu.VMEM((2, 4, 128), F32),
            pltpu.VMEM((4, 128), F32),
            pltpu.VMEM((1, 128), F32),
            pltpu.VMEM((COLUMN, 1, 128), F32),
            pltpu.VMEM((1, 128), F32),
            pltpu.VMEM((PLANE, 1, 128), F32),
            pltpu.VMEM((1, 128), F32),
            pltpu.SemaphoreType.DMA((2, 2)),
            pltpu.SemaphoreType.DMA((2,)),
            pltpu.SemaphoreType.DMA((5,)),
            pltpu.SemaphoreType.DMA((5,)),
            pltpu.SemaphoreType.REGULAR,
        ],
        compiler_params=pltpu.CompilerParams(collective_id=0, has_side_effects=True),
        name="perambulator",
    )(source_times, spin_dilution, eig, sol)
    return pl.pallas_call(
        finish,
        out_shape=results,
        in_specs=[vmem, vmem],
        out_specs=(hbm, hbm),
        scratch_shapes=[pltpu.SemaphoreType.DMA((2,))],
        compiler_params=pltpu.CompilerParams(vmem_limit_bytes=1 << 20),
        name="finish",
    )(pltpu.with_memory_space_constraint(block, pltpu.VMEM),
      pltpu.with_memory_space_constraint(norm, pltpu.VMEM))


def solution(mesh):
    finer = Mesh(mesh.devices.reshape(NY, NXL, NXH, NZ, NC), TA + SA)
    return jax.shard_map(
        on_device,
        mesh=finer,
        in_specs=(P(None, TA, None, None, SA), P(None, TA, None, None, None, None, SA), P(), P()),
        out_specs=(P(None, TA, SA), P()),
        check_vma=False,
    )
```

time: 36.5 us -> 31.7 us (0.87)
  local copies, waits for them, and re-layouts: 2.48 us -> 0 us
  Pallas kernels: 33.2 us -> 30.9 us
    unnamed x2 -> x0, local copies, waits for them, and re-layouts: 2.48 us -> none
    pallas_call x1 -> x2, Pallas kernels: 33.2 us -> 30.9 us  [the longest x1 30.3 us: on_device(): pl.pallas_call(kernel, out_shape=(pltpu.VMEM((2, 2, 128), F32), pltpu.VME...]
where the time goes in v2:
time: 31.7 us; the launch traced here: 31.5 us
  Pallas kernels  30.9 us (97%)
  between operations  0.64 us (2%)
    pallas_call x1, Pallas kernels, on_device(): pl.pallas_call(kernel, out_shape=(pltpu.VMEM((2, 2, 128), F32), pltpu.VME...  30.3 us

profile of v2, /device:TPU:1, one launch (start us, length us, event | category | flops | bytes accessed | tf_op | source)
XLA Modules:
  0.0 31.5 jit_solution(4047490998497496963)
XLA Ops:
  0.6 30.3 %perambulator.1 = (f32[2,2,128]{2,1,0:T(2,128)S(1)}, f32[3,8]{1,0:T(4,128)S(1)}) custom-call(s32[3]{0:T(128)} %times_ref.1, s32[3,8]{1,0:T(4,128)} %spin_ref.1, f32[2,2,3,64,512]{4,3,2,1,0:T(8,128)} %bitcast.5, f32[2,2,24,3,4,512]{5,4,3,2,1,0:T(4,128)} %bitcast.4), custom_call_target="tpu_custom_call" | custom-call | tf_op jit(solution)/shard_map/perambulator/pallas_call | solution.py:245
  30.9 0.6 %finish.1 = (f32[2,2,128]{2,1,0:T(2,128)}, f32[3,8]{1,0:T(4,128)}) custom-call(f32[2,2,128]{2,1,0:T(2,128)S(1)} %get-tuple-element.4.block_ref, f32[3,8]{1,0:T(4,128)S(1)} %get-tuple-element.5.norm_ref), custom_call_target="tpu_custom_call" | custom-call | tf_op jit(solution)/shard_map/finish/pallas_call | solution.py:272

commit v3 on v2

--- a/solution.py
+++ b/solution.py
@@ -14,6 +14,7 @@
 SA = ("xh", "z", "core")
 COLUMN = NZ * NC
 PLANE = NXH * NY * NXL
+LATE = 13
 
 
 def split(x):
@@ -26,70 +27,98 @@
     return lax.dot_general(a, b, (((1,), (1,)), ((), ())), preferred_element_type=F32)
 
 
-def kernel(times_ref, spin_ref, eig_hbm, sol_hbm, out_ref, norm_ref,
-           eig, sol, tmp, send, recv, half, other, row, rows1, total, rows2, final,
-           sol_sem, eig_sem, ssem, rsem, ready):
+def kernel(times_hbm, spin_hbm, eig_hbm, sol_hbm, out_ref, norm_ref,
+           eig, sol, times_ref, spin_ref, high, low, tmp, send, recv, half, other,
+           row, rows1, total, rows2, final,
+           sol_sem, eig_sem, int_sem, ssem, rsem, ready):
     y, xl, xh = lax.axis_index("y"), lax.axis_index("xl"), lax.axis_index("xh")
     z, core = lax.axis_index("z"), lax.axis_index("core")
-    me = z * NC + 1 - core
     plane_me = (xh * NY + y) * NXL + xl
-    is_root = me == 0
-
-    def sol_loads(p, t):
-        return [pltpu.make_async_copy(sol_hbm.at[p, t, :, c, :, pl.ds(128 * j, 128)],
-                                      sol.at[p, t, c, j], sol_sem.at[p, t])
-                for c in range(3) for j in range(4)]
-
-    def eig_loads(t):
-        return [pltpu.make_async_copy(eig_hbm.at[p, t], eig.at[p, t], eig_sem.at[t])
-                for p in range(2)]
+    place = z * NC + 1 - core
+    first = plane_me == 0
+    is_root = place == 0
+    is_spare = jnp.logical_and(first, place == 1)
+    shifted = jnp.where(place == 1, LATE, jnp.where(place <= LATE, place - 1, place))
+    me = jnp.where(jnp.logical_and(first, place >= 1), shifted, place)
+
+    def sol_load(p, t):
+        return pltpu.make_async_copy(sol_hbm.at[p, t], sol.at[p, t], sol_sem.at[p, t])
+
+    def eig_load(p, t):
+        return pltpu.make_async_copy(eig_hbm.at[p, t], eig.at[p, t], eig_sem.at[p, t])
 
     for t in range(2):
         for p in range(2):
-            for copy in sol_loads(p, t):
-                copy.start()
-    for t in range(2):
-        for copy in eig_loads(t):
-            copy.start()
+            sol_load(p, t).start()
+    for t in range(2):
+        for p in range(2):
+            eig_load(p, t).start()
+
+    int_loads = [pltpu.make_async_copy(times_hbm, times_ref, int_sem.at[0]),
+                 pltpu.make_async_copy(spin_hbm, spin_ref, int_sem.at[1])]
+    for copy in int_loads:
+        copy.start()
+
+    def at_place(n):
+        return {"z": n // NC, "core": 1 - lax.rem(n, NC)}
 
     def column(o):
-        return {"z": o // NC, "core": 1 - lax.rem(o, NC)}
-
-    def plane(i):
-        d = lax.rem(plane_me + i, PLANE)
-        return {"xh": d // (NY * NXL), "y": lax.rem(d // NXL, NY), "xl": lax.rem(d, NXL)}
+        moved = jnp.where(o == LATE, 1, jnp.where(o < LATE, o + 1, o))
+        return at_place(jnp.where(jnp.logical_and(first, o >= 1), moved, o))
+
+    def plane(d):
+        return {"xh": d // (NY * NXL), "y": lax.rem(d // NXL, NY), "xl": lax.rem(d, NXL),
+                "z": 0, "core": 1}
+
+    def each_plane(action):
+        @pl.loop(0, plane_me)
+        def _(d):
+            action(d)
+
+        @pl.loop(plane_me + 1, PLANE)
+        def _(d):
+            action(d)
 
     barrier = pltpu.get_barrier_semaphore()
+
+    def greet(device):
+        pl.semaphore_signal(barrier, inc=1, device_id=device, device_id_type=MESH)
 
     @pl.loop(me + 1, COLUMN)
     def _(o):
-        pl.semaphore_signal(barrier, inc=1, device_id=column(o), device_id_type=MESH)
-
-    pl.semaphore_signal(barrier, inc=1, device_id={"xh": 1 - xh}, device_id_type=MESH)
+        greet(column(o))
+
+    greet({"xh": 1 - xh})
 
     @pl.when(is_root)
     def _():
-        @pl.loop(1, PLANE)
-        def _(i):
-            pl.semaphore_signal(barrier, inc=1, device_id=plane(i), device_id_type=MESH)
-
-    squares = jnp.zeros((96, 128), F32)
+        each_plane(lambda d: greet(plane(d)))
+
+    @pl.when(is_spare)
+    def _():
+        @pl.loop(0, PLANE)
+        def _(d):
+            greet(plane(d))
+
+    high[...] = jnp.zeros(high.shape, BF16)
+    low[...] = jnp.zeros(low.shape, BF16)
+
+    pl.semaphore_wait(barrier, me + 1 + jnp.where(is_root, PLANE, 0))
+
+    @pl.loop(0, me)
+    def _(o):
+        pl.semaphore_signal(ready, inc=1, device_id=column(o), device_id_type=MESH)
+
+    squares = jnp.zeros((24, 4, 512), F32)
     for t in range(2):
         for p in range(2):
-            for copy in sol_loads(p, t):
-                copy.wait()
+            sol_load(p, t).wait()
             for c in range(3):
-                for j in range(4):
-                    piece = sol[p, t, c, j].reshape(96, 128)
-                    squares = squares + piece * piece
-        if t == 0:
-            pl.semaphore_wait(barrier, me + 1 + jnp.where(is_root, PLANE - 1, 0))
-
-            @pl.loop(0, me)
-            def _(o):
-                pl.semaphore_signal(ready, inc=1, device_id=column(o), device_id_type=MESH)
-
-    sums = jnp.sum(squares, axis=1, keepdims=True)
+                piece = sol[p, t, :, c]
+                squares = squares + piece * piece
+
+    lanes = (squares[:, :, :128] + squares[:, :, 128:256]) + (squares[:, :, 256:384] + squares[:, :, 384:])
+    sums = jnp.sum(lanes.reshape(96, 128), axis=1, keepdims=True)
     line = lax.broadcasted_iota(jnp.int32, (96, 128), 0)
     spot = lax.broadcasted_iota(jnp.int32, (96, 128), 1)
     row[...] = jnp.sum(jnp.where(line // 4 == spot, sums, F32(0)), axis=0, keepdims=True)
@@ -102,8 +131,18 @@
     def _():
         up.start()
 
+    for t in range(2):
+        for p in range(2):
+            for c in range(3):
+                h, l = split(sol[p, t, :, c].reshape(96, 512))
+                high[t, 128 * p:128 * p + 96, 512 * c:512 * c + 512] = h
+                low[t, 128 * p:128 * p + 96, 512 * c:512 * c + 512] = l
+
+    for copy in int_loads:
+        copy.wait()
     lane = lax.broadcasted_iota(jnp.int32, (1, 128), 1)
     lane16 = lax.broadcasted_iota(jnp.int32, (16, 128), 1)
+    signs = []
     for t in range(2):
         now = (y * NXL + xl) * 2 + t
         sign = jnp.ones((1, 128), F32)
@@ -112,20 +151,17 @@
             for k in range(8):
                 chir = jnp.where(spin_ref[s, k] < 2, F32(1), F32(-1))
                 sign = jnp.where(lane // 4 == s * 8 + k, edge * chir, sign)
-        for copy in eig_loads(t):
-            copy.wait()
-        prod = jnp.zeros((128, 256), F32)
-        for c in range(3):
-            e = jnp.concatenate([eig[0, t, c], eig[1, t, c]], axis=0)
-            parts = []
-            for p in range(2):
-                parts.append(jnp.concatenate(
-                    [sol[p, t, c, j].reshape(96, 128) for j in range(4)], axis=1))
-                parts.append(jnp.zeros((32, 512), F32))
-            s = jnp.concatenate(parts, axis=0)
-            eh, el = split(e)
-            sh, sl = split(s)
-            prod = prod + (dot_rows(eh, sh) + (dot_rows(eh, sl) + dot_rows(el, sh)))
+        signs.append(sign)
+
+    for t in range(2):
+        sign = signs[t]
+        eig_load(0, t).wait()
+        eig_load(1, t).wait()
+        e = jnp.concatenate(
+            [jnp.concatenate([eig[p, t, c] for c in range(3)], axis=1) for p in range(2)], axis=0)
+        eh, el = split(e)
+        both = dot_rows(jnp.concatenate([eh, el], axis=0), high[t])
+        prod = both[:128] + (both[128:] + dot_rows(eh, low[t]))
         real = (prod[:64, :128] + prod[64:, 128:]) * sign
         imag = (prod[:64, 128:] - prod[64:, :128]) * sign
         for p, part in enumerate((real, imag)):
@@ -142,9 +178,9 @@
 
     def send_block(o):
         peer = column(o)
-        place = pl.multiple_of((peer["z"] * NC + peer["core"]) * 8, 8)
+        spot = pl.multiple_of((peer["z"] * NC + peer["core"]) * 8, 8)
         pltpu.make_async_remote_copy(
-            src_ref=send.at[pl.ds(place, 8)], dst_ref=recv.at[me],
+            src_ref=send.at[pl.ds(spot, 8)], dst_ref=recv.at[me],
             send_sem=ssem.at[1], recv_sem=rsem.at[1],
             device_id=peer, device_id_type=MESH).start()
 
@@ -171,11 +207,24 @@
         arrived(rows1, COLUMN - 1, rsem.at[0])
         total[...] = jnp.sum(rows1[...], axis=0)
 
-        @pl.loop(1, PLANE)
-        def _(i):
+        def share(device):
             pltpu.make_async_remote_copy(
                 src_ref=total, dst_ref=rows2.at[plane_me], send_sem=ssem.at[2], recv_sem=rsem.at[2],
-                device_id=plane(i), device_id_type=MESH).start()
+                device_id=device, device_id_type=MESH).start()
+
+        @pl.when(jnp.logical_not(first))
+        def _():
+            share(plane(0))
+
+        share({"xh": 0, "y": 0, "xl": 0, "z": 0, "core": 0})
+
+        @pl.loop(1, plane_me)
+        def _(d):
+            share(plane(d))
+
+        @pl.loop(plane_me + 1, PLANE)
+        def _(d):
+            share(plane(d))
 
         rows2[plane_me] = total[...]
 
@@ -192,21 +241,40 @@
     out_ref[0] = mine[:2]
     out_ref[1] = mine[2:]
 
-    def down(o):
+    def down(n):
         return pltpu.make_async_remote_copy(
             src_ref=final, dst_ref=final, send_sem=ssem.at[4], recv_sem=rsem.at[4],
-            device_id=column(o), device_id_type=MESH)
+            device_id=at_place(n), device_id_type=MESH)
 
     @pl.when(is_root)
     def _():
         arrived(rows2, PLANE - 1, rsem.at[2])
+
+    @pl.when(is_spare)
+    def _():
+        arrived(rows2, PLANE, rsem.at[2])
+
+    summing = jnp.logical_or(is_root, is_spare)
+
+    @pl.when(summing)
+    def _():
         final[...] = jnp.sum(rows2[...], axis=0)
 
+    plain_root = jnp.logical_and(is_root, jnp.logical_not(first))
+
+    @pl.when(plain_root)
+    def _():
         @pl.loop(1, COLUMN)
-        def _(o):
-            down(o).start()
-
-    @pl.when(jnp.logical_not(is_root))
+        def _(n):
+            down(n).start()
+
+    @pl.when(is_spare)
+    def _():
+        @pl.loop(2, COLUMN)
+        def _(n):
+            down(n).start()
+
+    @pl.when(jnp.logical_not(summing))
     def _():
         down(0).wait_recv()
 
@@ -218,8 +286,15 @@
 
     @pl.when(is_root)
     def _():
-        arrived(rows2, PLANE - 1, ssem.at[2])
+        arrived(rows2, PLANE, ssem.at[2])
+
+    @pl.when(plain_root)
+    def _():
         arrived(rows1, COLUMN - 1, ssem.at[4])
+
+    @pl.when(is_spare)
+    def _():
+        arrived(rows1, COLUMN - 2, ssem.at[4])
 
     @pl.when(jnp.logical_not(is_root))
     def _():
@@ -239,17 +314,20 @@
     eig = jnp.transpose(eigvecs, (0, 1, 3, 2, 4))
     sol = jnp.transpose(solutions, (0, 1, 2, 3, 5, 4, 6)).reshape(2, 2, 24, 3, 4, 512)
     vmem = pl.BlockSpec(memory_space=pltpu.VMEM)
-    smem = pl.BlockSpec(memory_space=pltpu.SMEM)
     hbm = pl.BlockSpec(memory_space=pl.ANY)
     results = (jax.ShapeDtypeStruct((2, 2, 128), F32), jax.ShapeDtypeStruct((3, 8), F32))
     block, norm = pl.pallas_call(
         kernel,
         out_shape=(pltpu.VMEM((2, 2, 128), F32), pltpu.VMEM((3, 8), F32)),
-        in_specs=[smem, smem, hbm, hbm],
+        in_specs=[hbm, hbm, hbm, hbm],
         out_specs=(vmem, vmem),
         scratch_shapes=[
             pltpu.VMEM((2, 2, 3, 64, 512), F32),
-            pltpu.VMEM((2, 2, 3, 4, 24, 4, 128), F32),
+            pltpu.VMEM((2, 2, 24, 3, 4, 512), F32),
+            pltpu.SMEM((3,), jnp.int32),
+            pltpu.SMEM((3, 8), jnp.int32),
+            pltpu.VMEM((2, 256, 1536), BF16),
+            pltpu.VMEM((2, 256, 1536), BF16),
             pltpu.VMEM((64, 128), F32),
             pltpu.VMEM((COLUMN * 8, 128), F32),
             pltpu.VMEM((COLUMN, 8, 128), F32),
@@ -260,6 +338,7 @@
             pltpu.VMEM((1, 128), F32),
             pltpu.VMEM((PLANE, 1, 128), F32),
             pltpu.VMEM((1, 128), F32),
+            pltpu.SemaphoreType.DMA((2, 2)),
             pltpu.SemaphoreType.DMA((2, 2)),
             pltpu.SemaphoreType.DMA((2,)),
             pltpu.SemaphoreType.DMA((5,)),

time: 31.7 us -> 30.1 us (0.950); the launches traced: 31.5 us -> 29.5 us
  Pallas kernels: 30.9 us -> 28.9 us
    pallas_call x1, Pallas kernels: 30.3 us -> 28.3 us  [on_device(): pl.pallas_call(kernel, out_shape=(pltpu.VMEM((2, 2, 128), F32), pltpu.VME...]
where the time goes in v3:
time: 30.1 us; the launch traced here: 29.5 us
  Pallas kernels  28.9 us (96%)
  between operations  0.64 us (2%)
    pallas_call x1, Pallas kernels, on_device(): pl.pallas_call(kernel, out_shape=(pltpu.VMEM((2, 2, 128), F32), pltpu.VME...  28.3 us

profile of v3, /device:TPU:1, one launch (start us, length us, event | category | flops | bytes accessed | tf_op | source)
XLA Modules:
  0.0 29.5 jit_solution(3225822491333607698)
XLA Ops:
  0.6 28.3 %perambulator.1 = (f32[2,2,128]{2,1,0:T(2,128)S(1)}, f32[3,8]{1,0:T(4,128)S(1)}) custom-call(s32[3]{0:T(128)} %times_hbm.1, s32[3,8]{1,0:T(4,128)} %spin_hbm.1, f32[2,2,3,64,512]{4,3,2,1,0:T(8,128)} %bitcast.5, f32[2,2,24,3,4,512]{5,4,3,2,1,0:T(4,128)} %bitcast.4), custom_call_target="tpu_custom_call" | custom-call | tf_op jit(solution)/shard_map/perambulator/pallas_call | solution.py:319
  28.9 0.6 %finish.1 = (f32[2,2,128]{2,1,0:T(2,128)}, f32[3,8]{1,0:T(4,128)}) custom-call(f32[2,2,128]{2,1,0:T(2,128)S(1)} %get-tuple-element.4.block_ref, f32[3,8]{1,0:T(4,128)S(1)} %get-tuple-element.5.norm_ref), custom_call_target="tpu_custom_call" | custom-call | tf_op jit(solution)/shard_map/finish/pallas_call | solution.py:351

commit v4 on v3

--- a/solution.py
+++ b/solution.py
@@ -1,3 +1,5 @@
+import functools
+
 import jax
 import jax.numpy as jnp
 from jax import lax
@@ -15,6 +17,12 @@
 COLUMN = NZ * NC
 PLANE = NXH * NY * NXL
 LATE = 13
+GUESTS = 5
+RELAY = 4
+EARLY = (0, 1, 2, 16, 17)
+FAR_Y, FAR_LO, FAR_HI = 4, 10, 20
+FAR = FAR_HI - FAR_LO
+DIRECT = NXH * NXL * FAR
 
 
 def split(x):
@@ -29,7 +37,7 @@
 
 def kernel(times_hbm, spin_hbm, eig_hbm, sol_hbm, out_ref, norm_ref,
            eig, sol, times_ref, spin_ref, high, low, tmp, send, recv, half, other,
-           row, rows1, total, rows2, final,
+           row, rows1, near, total, rows2, rows3, final,
            sol_sem, eig_sem, int_sem, ssem, rsem, ready):
     y, xl, xh = lax.axis_index("y"), lax.axis_index("xl"), lax.axis_index("xh")
     z, core = lax.axis_index("z"), lax.axis_index("core")
@@ -37,22 +45,22 @@
     place = z * NC + 1 - core
     first = plane_me == 0
     is_root = place == 0
+    is_guest = jnp.logical_and(first, jnp.logical_and(place >= 1, place <= GUESTS))
     is_spare = jnp.logical_and(first, place == 1)
+    is_relay = jnp.logical_and(jnp.logical_not(first), place == RELAY)
     shifted = jnp.where(place == 1, LATE, jnp.where(place <= LATE, place - 1, place))
     me = jnp.where(jnp.logical_and(first, place >= 1), shifted, place)
-
-    def sol_load(p, t):
-        return pltpu.make_async_copy(sol_hbm.at[p, t], sol.at[p, t], sol_sem.at[p, t])
-
-    def eig_load(p, t):
-        return pltpu.make_async_copy(eig_hbm.at[p, t], eig.at[p, t], eig_sem.at[p, t])
-
-    for t in range(2):
-        for p in range(2):
-            sol_load(p, t).start()
-    for t in range(2):
-        for p in range(2):
-            eig_load(p, t).start()
+    in_far = y == FAR_Y
+    is_far = jnp.logical_and(in_far, jnp.logical_and(place >= FAR_LO, place < FAR_HI))
+    is_early = jnp.logical_and(is_root, functools.reduce(
+        jnp.logical_or, [plane_me == e for e in EARLY]))
+
+    for q in range(4):
+        pltpu.make_async_copy(sol_hbm.at[q % 2, q // 2], sol.at[q],
+                              sol_sem.at[q // 3]).start()
+    for q in range(4):
+        pltpu.make_async_copy(eig_hbm.at[q % 2, q // 2], eig.at[q % 2, q // 2],
+                              eig_sem).start()
 
     int_loads = [pltpu.make_async_copy(times_hbm, times_ref, int_sem.at[0]),
                  pltpu.make_async_copy(spin_hbm, spin_ref, int_sem.at[1])]
@@ -66,19 +74,13 @@
         moved = jnp.where(o == LATE, 1, jnp.where(o < LATE, o + 1, o))
         return at_place(jnp.where(jnp.logical_and(first, o >= 1), moved, o))
 
+    def plane_at(d):
+        return {"xh": d // (NY * NXL), "y": d // NXL % NY, "xl": d % NXL, "z": 0, "core": 1}
+
     def plane(d):
         return {"xh": d // (NY * NXL), "y": lax.rem(d // NXL, NY), "xl": lax.rem(d, NXL),
                 "z": 0, "core": 1}
 
-    def each_plane(action):
-        @pl.loop(0, plane_me)
-        def _(d):
-            action(d)
-
-        @pl.loop(plane_me + 1, PLANE)
-        def _(d):
-            action(d)
-
     barrier = pltpu.get_barrier_semaphore()
 
     def greet(device):
@@ -92,30 +94,47 @@
 
     @pl.when(is_root)
     def _():
-        each_plane(lambda d: greet(plane(d)))
-
-    @pl.when(is_spare)
+        @pl.loop(1, PLANE)
+        def _(i):
+            greet(plane(lax.rem(plane_me + i, PLANE)))
+
+    @pl.when(is_guest)
     def _():
         @pl.loop(0, PLANE)
         def _(d):
             greet(plane(d))
 
+    @pl.when(is_early)
+    def _():
+        @pl.loop(0, DIRECT)
+        def _(i):
+            n = FAR_LO + lax.rem(i, FAR)
+            greet({"xh": i // (NXL * FAR), "xl": lax.rem(i // FAR, NXL), "y": FAR_Y,
+                   "z": n // NC, "core": 1 - lax.rem(n, NC)})
+
     high[...] = jnp.zeros(high.shape, BF16)
     low[...] = jnp.zeros(low.shape, BF16)
 
-    pl.semaphore_wait(barrier, me + 1 + jnp.where(is_root, PLANE, 0))
+    pl.semaphore_wait(barrier, me + 1 + jnp.where(is_root, PLANE - 1 + GUESTS, 0)
+                      + jnp.where(is_far, len(EARLY), 0))
 
     @pl.loop(0, me)
     def _(o):
         pl.semaphore_signal(ready, inc=1, device_id=column(o), device_id_type=MESH)
 
     squares = jnp.zeros((24, 4, 512), F32)
-    for t in range(2):
-        for p in range(2):
-            sol_load(p, t).wait()
-            for c in range(3):
-                piece = sol[p, t, :, c]
-                squares = squares + piece * piece
+
+    def arrived(buf, count, sem):
+        pltpu.make_async_copy(buf.at[pl.ds(0, count)], buf.at[pl.ds(0, count)], sem).wait()
+
+    for q in range(4):
+        if q == 0:
+            arrived(sol, 3, sol_sem.at[0])
+        if q == 3:
+            arrived(sol, 1, sol_sem.at[1])
+        for c in range(3):
+            piece = sol[q, :, c]
+            squares = squares + piece * piece
 
     lanes = (squares[:, :, :128] + squares[:, :, 128:256]) + (squares[:, :, 256:384] + squares[:, :, 384:])
     sums = jnp.sum(lanes.reshape(96, 128), axis=1, keepdims=True)
@@ -123,23 +142,32 @@
     spot = lax.broadcasted_iota(jnp.int32, (96, 128), 1)
     row[...] = jnp.sum(jnp.where(line // 4 == spot, sums, F32(0)), axis=0, keepdims=True)
 
-    up = pltpu.make_async_remote_copy(
-        src_ref=row, dst_ref=rows1.at[me], send_sem=ssem.at[0], recv_sem=rsem.at[0],
-        device_id={"z": 0, "core": 1}, device_id_type=MESH)
-
-    @pl.when(jnp.logical_not(is_root))
-    def _():
-        up.start()
+    def send_row(slot, sem, device):
+        pltpu.make_async_remote_copy(
+            src_ref=row, dst_ref=slot, send_sem=ssem, recv_sem=sem,
+            device_id=device, device_id_type=MESH).start()
+
+    @pl.when(is_far)
+    def _():
+        spot = (xh * NXL + xl) * FAR + place - FAR_LO
+        for e in EARLY:
+            send_row(rows3.at[spot], rsem.at[4], plane_at(e))
+        send_row(rows1.at[me], rsem.at[4], {"z": 0, "core": 1})
+
+    @pl.when(jnp.logical_not(jnp.logical_or(is_root, is_far)))
+    def _():
+        send_row(rows1.at[me], rsem.at[0], {"z": 0, "core": 1})
 
     for t in range(2):
         for p in range(2):
             for c in range(3):
-                h, l = split(sol[p, t, :, c].reshape(96, 512))
+                h, l = split(sol[2 * t + p, :, c].reshape(96, 512))
                 high[t, 128 * p:128 * p + 96, 512 * c:512 * c + 512] = h
                 low[t, 128 * p:128 * p + 96, 512 * c:512 * c + 512] = l
 
     for copy in int_loads:
         copy.wait()
+    pltpu.make_async_copy(eig, eig, eig_sem).wait()
     lane = lax.broadcasted_iota(jnp.int32, (1, 128), 1)
     lane16 = lax.broadcasted_iota(jnp.int32, (16, 128), 1)
     signs = []
@@ -155,8 +183,6 @@
 
     for t in range(2):
         sign = signs[t]
-        eig_load(0, t).wait()
-        eig_load(1, t).wait()
         e = jnp.concatenate(
             [jnp.concatenate([eig[p, t, c] for c in range(3)], axis=1) for p in range(2)], axis=0)
         eh, el = split(e)
@@ -181,7 +207,7 @@
         spot = pl.multiple_of((peer["z"] * NC + peer["core"]) * 8, 8)
         pltpu.make_async_remote_copy(
             src_ref=send.at[pl.ds(spot, 8)], dst_ref=recv.at[me],
-            send_sem=ssem.at[1], recv_sem=rsem.at[1],
+            send_sem=ssem, recv_sem=rsem.at[1],
             device_id=peer, device_id_type=MESH).start()
 
     @pl.loop(0, me)
@@ -198,33 +224,47 @@
 
     recv[me] = send[pl.ds(pl.multiple_of((z * NC + core) * 8, 8), 8), :]
 
-    def arrived(buf, count, sem):
-        pltpu.make_async_copy(buf.at[pl.ds(0, count)], buf.at[pl.ds(0, count)], sem).wait()
+    def share(source, device):
+        pltpu.make_async_remote_copy(
+            src_ref=source, dst_ref=rows2.at[plane_me], send_sem=ssem, recv_sem=rsem.at[2],
+            device_id=device, device_id_type=MESH).start()
+
+    def share_early(source):
+        for e in EARLY:
+            @pl.when(plane_me != e)
+            def _():
+                share(source, plane_at(e))
 
     @pl.when(is_root)
     def _():
         rows1[0] = row[...]
+
+    @pl.when(jnp.logical_and(is_root, in_far))
+    def _():
+        arrived(rows1, COLUMN - 1 - FAR, rsem.at[0])
+        near[...] = (jnp.sum(rows1[0:FAR_LO], axis=0)
+                     + jnp.sum(rows1[FAR_HI:COLUMN], axis=0))
+        share_early(near)
+        arrived(rows1, FAR, rsem.at[4])
+        total[...] = near[...] + jnp.sum(rows1[FAR_LO:FAR_HI], axis=0)
+
+    @pl.when(jnp.logical_and(is_root, jnp.logical_not(in_far)))
+    def _():
         arrived(rows1, COLUMN - 1, rsem.at[0])
-        total[...] = jnp.sum(rows1[...], axis=0)
-
-        def share(device):
-            pltpu.make_async_remote_copy(
-                src_ref=total, dst_ref=rows2.at[plane_me], send_sem=ssem.at[2], recv_sem=rsem.at[2],
-                device_id=device, device_id_type=MESH).start()
-
-        @pl.when(jnp.logical_not(first))
-        def _():
-            share(plane(0))
-
-        share({"xh": 0, "y": 0, "xl": 0, "z": 0, "core": 0})
-
-        @pl.loop(1, plane_me)
-        def _(d):
-            share(plane(d))
-
-        @pl.loop(plane_me + 1, PLANE)
-        def _(d):
-            share(plane(d))
+        total[...] = jnp.sum(rows1[0:COLUMN], axis=0)
+        share_early(total)
+
+    @pl.when(is_root)
+    def _():
+        for n in range(1, GUESTS + 1):
+            share(total, {"xh": 0, "y": 0, "xl": 0, "z": n // NC, "core": 1 - n % NC})
+
+        for low_end, high_end in ((3, 16), (18, 32)):
+            @pl.loop(low_end, high_end)
+            def _(d):
+                @pl.when(d != plane_me)
+                def _():
+                    share(total, plane(d))
 
         rows2[plane_me] = total[...]
 
@@ -233,72 +273,76 @@
     half[0] = block[:4]
     half[1] = block[4:]
     cross = pltpu.make_async_remote_copy(
-        src_ref=half.at[1 - xh], dst_ref=other, send_sem=ssem.at[3], recv_sem=rsem.at[3],
+        src_ref=half.at[1 - xh], dst_ref=other, send_sem=ssem, recv_sem=rsem.at[3],
         device_id={"xh": 1 - xh}, device_id_type=MESH)
     cross.start()
-    cross.wait()
+    cross.wait_recv()
     mine = half[xh] + other[...]
     out_ref[0] = mine[:2]
     out_ref[1] = mine[2:]
 
     def down(n):
         return pltpu.make_async_remote_copy(
-            src_ref=final, dst_ref=final, send_sem=ssem.at[4], recv_sem=rsem.at[4],
+            src_ref=final, dst_ref=final, send_sem=ssem, recv_sem=rsem.at[0],
             device_id=at_place(n), device_id_type=MESH)
 
     @pl.when(is_root)
     def _():
         arrived(rows2, PLANE - 1, rsem.at[2])
 
-    @pl.when(is_spare)
+    @pl.when(is_guest)
     def _():
         arrived(rows2, PLANE, rsem.at[2])
 
-    summing = jnp.logical_or(is_root, is_spare)
+    summing = jnp.logical_or(is_root, is_guest)
 
     @pl.when(summing)
     def _():
         final[...] = jnp.sum(rows2[...], axis=0)
 
+    @pl.when(is_early)
+    def _():
+        arrived(rows3, DIRECT, rsem.at[4])
+        final[...] = final[...] + jnp.sum(rows3[...], axis=0)
+
+    @pl.when(jnp.logical_not(summing))
+    def _():
+        down(0).wait_recv()
+
     plain_root = jnp.logical_and(is_root, jnp.logical_not(first))
 
     @pl.when(plain_root)
     def _():
-        @pl.loop(1, COLUMN)
+        for n in range(1, RELAY + 1):
+            down(n).start()
+
+    @pl.when(is_relay)
+    def _():
+        @pl.loop(RELAY + 1, COLUMN)
         def _(n):
             down(n).start()
 
     @pl.when(is_spare)
     def _():
-        @pl.loop(2, COLUMN)
+        @pl.loop(GUESTS + 1, COLUMN)
         def _(n):
             down(n).start()
-
-    @pl.when(jnp.logical_not(summing))
-    def _():
-        down(0).wait_recv()
 
     norm = final[...] / F32(9437184.0)
     for s in range(3):
         norm_ref[s:s + 1, :] = pltpu.roll(norm, (128 - 8 * s) % 128, 1)[:, :8]
 
-    arrived(recv, COLUMN - 1, ssem.at[1])
-
-    @pl.when(is_root)
-    def _():
-        arrived(rows2, PLANE, ssem.at[2])
-
-    @pl.when(plain_root)
-    def _():
-        arrived(rows1, COLUMN - 1, ssem.at[4])
-
-    @pl.when(is_spare)
-    def _():
-        arrived(rows1, COLUMN - 2, ssem.at[4])
-
-    @pl.when(jnp.logical_not(is_root))
-    def _():
-        up.wait_send()
+    base = 8 * (COLUMN - 1) + 4
+    roles = ((jnp.logical_and(is_root, first), PLANE - 1 + GUESTS),
+             (plain_root, PLANE - 1 + GUESTS + RELAY),
+             (is_relay, COLUMN - RELAY),
+             (is_spare, COLUMN - GUESTS),
+             (is_far, 1 + len(EARLY)))
+    rest = True
+    for role, count in roles:
+        pl.when(role)(functools.partial(arrived, rows1, base + count, ssem))
+        rest = jnp.logical_and(rest, jnp.logical_not(role))
+    pl.when(rest)(functools.partial(arrived, rows1, base + 1, ssem))
 
 
 def finish(block_ref, norm_ref, block_out, norm_out, sem):
@@ -323,7 +367,7 @@
         out_specs=(vmem, vmem),
         scratch_shapes=[
             pltpu.VMEM((2, 2, 3, 64, 512), F32),
-            pltpu.VMEM((2, 2, 24, 3, 4, 512), F32),
+            pltpu.VMEM((4, 24, 3, 4, 512), F32),
             pltpu.SMEM((3,), jnp.int32),
             pltpu.SMEM((3, 8), jnp.int32),
             pltpu.VMEM((2, 256, 1536), BF16),
@@ -334,14 +378,16 @@
             pltpu.VMEM((2, 4, 128), F32),
             pltpu.VMEM((4, 128), F32),
             pltpu.VMEM((1, 128), F32),
-            pltpu.VMEM((COLUMN, 1, 128), F32),
+            pltpu.VMEM((256, 1, 128), F32),
+            pltpu.VMEM((1, 128), F32),
             pltpu.VMEM((1, 128), F32),
             pltpu.VMEM((PLANE, 1, 128), F32),
+            pltpu.VMEM((DIRECT, 1, 128), F32),
             pltpu.VMEM((1, 128), F32),
-            pltpu.SemaphoreType.DMA((2, 2)),
-            pltpu.SemaphoreType.DMA((2, 2)),
             pltpu.SemaphoreType.DMA((2,)),
-            pltpu.SemaphoreType.DMA((5,)),
+            pltpu.SemaphoreType.DMA,
+            pltpu.SemaphoreType.DMA((2,)),
+            pltpu.SemaphoreType.DMA,
             pltpu.SemaphoreType.DMA((5,)),
             pltpu.SemaphoreType.REGULAR,
         ],

time: 30.1 us -> 29.2 us (0.970); the launches traced: 29.5 us -> 29 us
  Pallas kernels: 28.9 us -> 28.4 us
    pallas_call x1, Pallas kernels: 28.3 us -> 27.8 us  [on_device(): pl.pallas_call(kernel, out_shape=(pltpu.VMEM((2, 2, 128), F32), pltpu.VME...]
where the time goes in v4:
time: 29.2 us; the launch traced here: 29 us
  Pallas kernels  28.4 us (97%)
  between operations  0.64 us (2%)
    pallas_call x1, Pallas kernels, on_device(): pl.pallas_call(kernel, out_shape=(pltpu.VMEM((2, 2, 128), F32), pltpu.VME...  27.8 us
    pallas_call x1, Pallas kernels, on_device(): pl.pallas_call(finish, out_shape=results, in_specs=[vmem, vmem], out_spec...  0.6 us

profile of v4, /device:TPU:1, one launch (start us, length us, event | category | flops | bytes accessed | tf_op | source)
XLA Modules:
  0.0 29.0 jit_solution(171620178286524227)
XLA Ops:
  0.6 27.8 %perambulator.1 = (f32[2,2,128]{2,1,0:T(2,128)S(1)}, f32[3,8]{1,0:T(4,128)S(1)}) custom-call(s32[3]{0:T(128)} %times_hbm.1, s32[3,8]{1,0:T(4,128)} %spin_hbm.1, f32[2,2,3,64,512]{4,3,2,1,0:T(8,128)} %bitcast.5, f32[2,2,24,3,4,512]{5,4,3,2,1,0:T(4,128)} %bitcast.4), custom_call_target="tpu_custom_call" | custom-call | tf_op jit(solution)/shard_map/perambulator/pallas_call | solution.py:363
  28.4 0.6 %finish.1 = (f32[2,2,128]{2,1,0:T(2,128)}, f32[3,8]{1,0:T(4,128)}) custom-call(f32[2,2,128]{2,1,0:T(2,128)S(1)} %get-tuple-element.4.block_ref, f32[3,8]{1,0:T(4,128)S(1)} %get-tuple-element.5.norm_ref), custom_call_target="tpu_custom_call" | custom-call | tf_op jit(solution)/shard_map/finish/pallas_call | solution.py:397

commit v5 on v4

--- a/solution.py
+++ b/solution.py
@@ -17,12 +17,12 @@
 COLUMN = NZ * NC
 PLANE = NXH * NY * NXL
 LATE = 13
-GUESTS = 5
+GUESTS = 7
 RELAY = 4
 EARLY = (0, 1, 2, 16, 17)
-FAR_Y, FAR_LO, FAR_HI = 4, 10, 20
-FAR = FAR_HI - FAR_LO
-DIRECT = NXH * NXL * FAR
+FAR_Y, FAR_YS, FAR_LO = 4, 2, 10
+FAR = COLUMN - FAR_LO
+DIRECT = NXH * NXL * FAR_YS * FAR
 
 
 def split(x):
@@ -50,8 +50,8 @@
     is_relay = jnp.logical_and(jnp.logical_not(first), place == RELAY)
     shifted = jnp.where(place == 1, LATE, jnp.where(place <= LATE, place - 1, place))
     me = jnp.where(jnp.logical_and(first, place >= 1), shifted, place)
-    in_far = y == FAR_Y
-    is_far = jnp.logical_and(in_far, jnp.logical_and(place >= FAR_LO, place < FAR_HI))
+    in_far = jnp.logical_and(y >= FAR_Y, y < FAR_Y + FAR_YS)
+    is_far = jnp.logical_and(in_far, place >= FAR_LO)
     is_early = jnp.logical_and(is_root, functools.reduce(
         jnp.logical_or, [plane_me == e for e in EARLY]))
 
@@ -109,7 +109,8 @@
         @pl.loop(0, DIRECT)
         def _(i):
             n = FAR_LO + lax.rem(i, FAR)
-            greet({"xh": i // (NXL * FAR), "xl": lax.rem(i // FAR, NXL), "y": FAR_Y,
+            greet({"xh": i // (NXL * FAR_YS * FAR), "xl": lax.rem(i // (FAR_YS * FAR), NXL),
+                   "y": FAR_Y + lax.rem(i // FAR, FAR_YS),
                    "z": n // NC, "core": 1 - lax.rem(n, NC)})
 
     high[...] = jnp.zeros(high.shape, BF16)
@@ -149,10 +150,11 @@
 
     @pl.when(is_far)
     def _():
-        spot = (xh * NXL + xl) * FAR + place - FAR_LO
-        for e in EARLY:
+        spot = ((xh * NXL + xl) * FAR_YS + y - FAR_Y) * FAR + place - FAR_LO
+        send_row(rows3.at[spot], rsem.at[4], plane_at(EARLY[0]))
+        send_row(rows1.at[me], rsem.at[4], {"z": 0, "core": 1})
+        for e in EARLY[1:]:
             send_row(rows3.at[spot], rsem.at[4], plane_at(e))
-        send_row(rows1.at[me], rsem.at[4], {"z": 0, "core": 1})
 
     @pl.when(jnp.logical_not(jnp.logical_or(is_root, is_far)))
     def _():
@@ -191,7 +193,7 @@
         real = (prod[:64, :128] + prod[64:, 128:]) * sign
         imag = (prod[:64, 128:] - prod[64:, :128]) * sign
         for p, part in enumerate((real, imag)):
-            tmp[...] = part
+            tmp[:64] = part
             a0 = tmp[pl.ds(0, 16, stride=4), :]
             r1 = pltpu.roll(tmp[pl.ds(1, 16, stride=4), :], 96, 1)
             r2 = pltpu.roll(tmp[pl.ds(2, 16, stride=4), :], 64, 1)
@@ -214,16 +216,6 @@
     def _(o):
         send_block(o)
 
-    @pl.when(me < COLUMN - 1)
-    def _():
-        pl.semaphore_wait(ready, COLUMN - 1 - me)
-
-    @pl.loop(me + 1, COLUMN)
-    def _(o):
-        send_block(o)
-
-    recv[me] = send[pl.ds(pl.multiple_of((z * NC + core) * 8, 8), 8), :]
-
     def share(source, device):
         pltpu.make_async_remote_copy(
             src_ref=source, dst_ref=rows2.at[plane_me], send_sem=ssem, recv_sem=rsem.at[2],
@@ -235,18 +227,32 @@
             def _():
                 share(source, plane_at(e))
 
+    is_far_root = jnp.logical_and(is_root, in_far)
+
     @pl.when(is_root)
     def _():
         rows1[0] = row[...]
 
-    @pl.when(jnp.logical_and(is_root, in_far))
-    def _():
-        arrived(rows1, COLUMN - 1 - FAR, rsem.at[0])
-        near[...] = (jnp.sum(rows1[0:FAR_LO], axis=0)
-                     + jnp.sum(rows1[FAR_HI:COLUMN], axis=0))
+    @pl.when(is_far_root)
+    def _():
+        arrived(rows1, FAR_LO - 1, rsem.at[0])
+        near[...] = jnp.sum(rows1[0:FAR_LO], axis=0)
         share_early(near)
+
+    @pl.when(me < COLUMN - 1)
+    def _():
+        pl.semaphore_wait(ready, COLUMN - 1 - me)
+
+    @pl.loop(me + 1, COLUMN)
+    def _(o):
+        send_block(o)
+
+    recv[me] = send[pl.ds(pl.multiple_of((z * NC + core) * 8, 8), 8), :]
+
+    @pl.when(is_far_root)
+    def _():
         arrived(rows1, FAR, rsem.at[4])
-        total[...] = near[...] + jnp.sum(rows1[FAR_LO:FAR_HI], axis=0)
+        total[...] = near[...] + jnp.sum(rows1[FAR_LO:COLUMN], axis=0)
 
     @pl.when(jnp.logical_and(is_root, jnp.logical_not(in_far)))
     def _():
@@ -372,8 +378,8 @@
             pltpu.SMEM((3, 8), jnp.int32),
             pltpu.VMEM((2, 256, 1536), BF16),
             pltpu.VMEM((2, 256, 1536), BF16),
-            pltpu.VMEM((64, 128), F32),
-            pltpu.VMEM((COLUMN * 8, 128), F32),
+            pltpu.VMEM((72, 128), F32),
+            pltpu.VMEM((COLUMN * 8 + 24, 128), F32),
             pltpu.VMEM((COLUMN, 8, 128), F32),
             pltpu.VMEM((2, 4, 128), F32),
             pltpu.VMEM((4, 128), F32),

time: 29.2 us -> 28.4 us (0.973)
  Pallas kernels: 28.4 us -> 27.7 us
    pallas_call x1, Pallas kernels: 27.8 us -> 27.1 us  [on_device(): pl.pallas_call(kernel, out_shape=(pltpu.VMEM((2, 2, 128), F32), pltpu.VME...]
where the time goes in v5:
time: 28.4 us; the launch traced here: 28.3 us
  Pallas kernels  27.7 us (98%)
  between operations  0.64 us (2%)
    pallas_call x1, Pallas kernels, on_device(): pl.pallas_call(kernel, out_shape=(pltpu.VMEM((2, 2, 128), F32), pltpu.VME...  27.1 us
    pallas_call x1, Pallas kernels, on_device(): pl.pallas_call(finish, out_shape=results, in_specs=[vmem, vmem], out_spec...  0.6 us

profile of v5, /device:TPU:1, one launch (start us, length us, event | category | flops | bytes accessed | tf_op | source)
XLA Modules:
  0.0 28.3 jit_solution(12861098772095955288)
XLA Ops:
  0.6 27.1 %perambulator.1 = (f32[2,2,128]{2,1,0:T(2,128)S(1)}, f32[3,8]{1,0:T(4,128)S(1)}) custom-call(s32[3]{0:T(128)} %times_hbm.1, s32[3,8]{1,0:T(4,128)} %spin_hbm.1, f32[2,2,3,64,512]{4,3,2,1,0:T(8,128)} %bitcast.5, f32[2,2,24,3,4,512]{5,4,3,2,1,0:T(4,128)} %bitcast.4), custom_call_target="tpu_custom_call" | custom-call | tf_op jit(solution)/shard_map/perambulator/pallas_call | solution.py:369
  27.7 0.6 %finish.1 = (f32[2,2,128]{2,1,0:T(2,128)}, f32[3,8]{1,0:T(4,128)}) custom-call(f32[2,2,128]{2,1,0:T(2,128)S(1)} %get-tuple-element.4.block_ref, f32[3,8]{1,0:T(4,128)S(1)} %get-tuple-element.5.norm_ref), custom_call_target="tpu_custom_call" | custom-call | tf_op jit(solution)/shard_map/finish/pallas_call | solution.py:403

commit v6 on v5

--- a/solution.py
+++ b/solution.py
@@ -19,7 +19,9 @@
 LATE = 13
 GUESTS = 7
 RELAY = 4
-EARLY = (0, 1, 2, 16, 17)
+EARLY = (0, 1, 16, 17, 2, 3, 18, 19)
+DIRECT_GUESTS = (2, 3)
+OTHERS = ((4, 16), (20, 32))
 FAR_Y, FAR_YS, FAR_LO = 4, 2, 10
 FAR = COLUMN - FAR_LO
 DIRECT = NXH * NXL * FAR_YS * FAR
@@ -37,7 +39,7 @@
 
 def kernel(times_hbm, spin_hbm, eig_hbm, sol_hbm, out_ref, norm_ref,
            eig, sol, times_ref, spin_ref, high, low, tmp, send, recv, half, other,
-           row, rows1, near, total, rows2, rows3, final,
+           row, rows1, near, total, rows2, rows3, final, tally,
            sol_sem, eig_sem, int_sem, ssem, rsem, ready):
     y, xl, xh = lax.axis_index("y"), lax.axis_index("xl"), lax.axis_index("xh")
     z, core = lax.axis_index("z"), lax.axis_index("core")
@@ -52,16 +54,15 @@
     me = jnp.where(jnp.logical_and(first, place >= 1), shifted, place)
     in_far = jnp.logical_and(y >= FAR_Y, y < FAR_Y + FAR_YS)
     is_far = jnp.logical_and(in_far, place >= FAR_LO)
-    is_early = jnp.logical_and(is_root, functools.reduce(
-        jnp.logical_or, [plane_me == e for e in EARLY]))
+    is_early = jnp.logical_or(
+        jnp.logical_and(is_root, functools.reduce(
+            jnp.logical_or, [plane_me == e for e in EARLY])),
+        jnp.logical_and(first, functools.reduce(
+            jnp.logical_or, [place == n for n in DIRECT_GUESTS])))
 
     for q in range(4):
         pltpu.make_async_copy(sol_hbm.at[q % 2, q // 2], sol.at[q],
                               sol_sem.at[q // 3]).start()
-    for q in range(4):
-        pltpu.make_async_copy(eig_hbm.at[q % 2, q // 2], eig.at[q % 2, q // 2],
-                              eig_sem).start()
-
     int_loads = [pltpu.make_async_copy(times_hbm, times_ref, int_sem.at[0]),
                  pltpu.make_async_copy(spin_hbm, spin_ref, int_sem.at[1])]
     for copy in int_loads:
@@ -76,6 +77,9 @@
 
     def plane_at(d):
         return {"xh": d // (NY * NXL), "y": d // NXL % NY, "xl": d % NXL, "z": 0, "core": 1}
+
+    def guest(n):
+        return {"xh": 0, "y": 0, "xl": 0, "z": n // NC, "core": 1 - n % NC}
 
     def plane(d):
         return {"xh": d // (NY * NXL), "y": lax.rem(d // NXL, NY), "xl": lax.rem(d, NXL),
@@ -117,7 +121,7 @@
     low[...] = jnp.zeros(low.shape, BF16)
 
     pl.semaphore_wait(barrier, me + 1 + jnp.where(is_root, PLANE - 1 + GUESTS, 0)
-                      + jnp.where(is_far, len(EARLY), 0))
+                      + jnp.where(is_far, len(EARLY) + len(DIRECT_GUESTS), 0))
 
     @pl.loop(0, me)
     def _(o):
@@ -151,14 +155,20 @@
     @pl.when(is_far)
     def _():
         spot = ((xh * NXL + xl) * FAR_YS + y - FAR_Y) * FAR + place - FAR_LO
-        send_row(rows3.at[spot], rsem.at[4], plane_at(EARLY[0]))
-        send_row(rows1.at[me], rsem.at[4], {"z": 0, "core": 1})
+        send_row(rows3.at[pl.ds(spot, 1)], rsem.at[4], plane_at(EARLY[0]))
+        send_row(rows1.at[pl.ds(me, 1)], rsem.at[4], {"z": 0, "core": 1})
+        for n in DIRECT_GUESTS:
+            send_row(rows3.at[pl.ds(spot, 1)], rsem.at[4], guest(n))
         for e in EARLY[1:]:
-            send_row(rows3.at[spot], rsem.at[4], plane_at(e))
+            send_row(rows3.at[pl.ds(spot, 1)], rsem.at[4], plane_at(e))
 
     @pl.when(jnp.logical_not(jnp.logical_or(is_root, is_far)))
     def _():
-        send_row(rows1.at[me], rsem.at[0], {"z": 0, "core": 1})
+        send_row(rows1.at[pl.ds(me, 1)], rsem.at[0], {"z": 0, "core": 1})
+
+    for q in range(4):
+        pltpu.make_async_copy(eig_hbm.at[q % 2, q // 2], eig.at[q % 2, q // 2],
+                              eig_sem).start()
 
     for t in range(2):
         for p in range(2):
@@ -218,7 +228,7 @@
 
     def share(source, device):
         pltpu.make_async_remote_copy(
-            src_ref=source, dst_ref=rows2.at[plane_me], send_sem=ssem, recv_sem=rsem.at[2],
+            src_ref=source, dst_ref=rows2.at[pl.ds(plane_me, 1)], send_sem=ssem, recv_sem=rsem.at[2],
             device_id=device, device_id_type=MESH).start()
 
     def share_early(source):
@@ -227,16 +237,19 @@
             def _():
                 share(source, plane_at(e))
 
+        for n in DIRECT_GUESTS:
+            share(source, guest(n))
+
     is_far_root = jnp.logical_and(is_root, in_far)
 
     @pl.when(is_root)
     def _():
-        rows1[0] = row[...]
+        rows1[0:1] = row[...]
 
     @pl.when(is_far_root)
     def _():
-        arrived(rows1, FAR_LO - 1, rsem.at[0])
-        near[...] = jnp.sum(rows1[0:FAR_LO], axis=0)
+        arrived(tally, FAR_LO - 1, rsem.at[0])
+        near[...] = jnp.sum(rows1[0:FAR_LO], axis=0, keepdims=True)
         share_early(near)
 
     @pl.when(me < COLUMN - 1)
@@ -251,28 +264,29 @@
 
     @pl.when(is_far_root)
     def _():
-        arrived(rows1, FAR, rsem.at[4])
-        total[...] = near[...] + jnp.sum(rows1[FAR_LO:COLUMN], axis=0)
+        arrived(tally, FAR, rsem.at[4])
+        total[...] = near[...] + jnp.sum(rows1[FAR_LO:COLUMN], axis=0, keepdims=True)
 
     @pl.when(jnp.logical_and(is_root, jnp.logical_not(in_far)))
     def _():
-        arrived(rows1, COLUMN - 1, rsem.at[0])
-        total[...] = jnp.sum(rows1[0:COLUMN], axis=0)
+        arrived(tally, COLUMN - 1, rsem.at[0])
+        total[...] = jnp.sum(rows1[0:COLUMN], axis=0, keepdims=True)
         share_early(total)
 
     @pl.when(is_root)
     def _():
         for n in range(1, GUESTS + 1):
-            share(total, {"xh": 0, "y": 0, "xl": 0, "z": n // NC, "core": 1 - n % NC})
-
-        for low_end, high_end in ((3, 16), (18, 32)):
+            if n not in DIRECT_GUESTS:
+                share(total, guest(n))
+
+        for low_end, high_end in OTHERS:
             @pl.loop(low_end, high_end)
             def _(d):
                 @pl.when(d != plane_me)
                 def _():
                     share(total, plane(d))
 
-        rows2[plane_me] = total[...]
+        rows2[pl.ds(plane_me, 1)] = total[...]
 
     arrived(recv, COLUMN - 1, rsem.at[1])
     block = jnp.sum(recv[...], axis=0)
@@ -294,22 +308,22 @@
 
     @pl.when(is_root)
     def _():
-        arrived(rows2, PLANE - 1, rsem.at[2])
+        arrived(tally, PLANE - 1, rsem.at[2])
 
     @pl.when(is_guest)
     def _():
-        arrived(rows2, PLANE, rsem.at[2])
+        arrived(tally, PLANE, rsem.at[2])
 
     summing = jnp.logical_or(is_root, is_guest)
 
     @pl.when(summing)
     def _():
-        final[...] = jnp.sum(rows2[...], axis=0)
+        final[...] = jnp.sum(rows2[...], axis=0, keepdims=True)
 
     @pl.when(is_early)
     def _():
-        arrived(rows3, DIRECT, rsem.at[4])
-        final[...] = final[...] + jnp.sum(rows3[...], axis=0)
+        arrived(tally, DIRECT, rsem.at[4])
+        final[...] = final[...] + jnp.sum(rows3[...], axis=0, keepdims=True)
 
     @pl.when(jnp.logical_not(summing))
     def _():
@@ -334,7 +348,7 @@
         def _(n):
             down(n).start()
 
-    norm = final[...] / F32(9437184.0)
+    norm = final[...] * F32(1 / 9437184.0)
     for s in range(3):
         norm_ref[s:s + 1, :] = pltpu.roll(norm, (128 - 8 * s) % 128, 1)[:, :8]
 
@@ -343,12 +357,12 @@
              (plain_root, PLANE - 1 + GUESTS + RELAY),
              (is_relay, COLUMN - RELAY),
              (is_spare, COLUMN - GUESTS),
-             (is_far, 1 + len(EARLY)))
+             (is_far, 1 + len(EARLY) + len(DIRECT_GUESTS)))
     rest = True
     for role, count in roles:
-        pl.when(role)(functools.partial(arrived, rows1, base + count, ssem))
+        pl.when(role)(functools.partial(arrived, tally, base + count, ssem))
         rest = jnp.logical_and(rest, jnp.logical_not(role))
-    pl.when(rest)(functools.partial(arrived, rows1, base + 1, ssem))
+    pl.when(rest)(functools.partial(arrived, tally, base + 1, ssem))
 
 
 def finish(block_ref, norm_ref, block_out, norm_out, sem):
@@ -384,12 +398,13 @@
             pltpu.VMEM((2, 4, 128), F32),
             pltpu.VMEM((4, 128), F32),
             pltpu.VMEM((1, 128), F32),
-            pltpu.VMEM((256, 1, 128), F32),
+            pltpu.VMEM((COLUMN, 128), F32),
             pltpu.VMEM((1, 128), F32),
             pltpu.VMEM((1, 128), F32),
-            pltpu.VMEM((PLANE, 1, 128), F32),
-            pltpu.VMEM((DIRECT, 1, 128), F32),
+            pltpu.VMEM((PLANE, 128), F32),
+            pltpu.VMEM((DIRECT, 128), F32),
             pltpu.VMEM((1, 128), F32),
+            pltpu.VMEM((256, 1, 128), F32),
             pltpu.SemaphoreType.DMA((2,)),
             pltpu.SemaphoreType.DMA,
             pltpu.SemaphoreType.DMA((2,)),

time: 28.4 us -> 28 us (0.986)
  Pallas kernels: 27.7 us -> 27.2 us
    pallas_call x1, Pallas kernels: 27.1 us -> 26.6 us  [on_device(): pl.pallas_call(kernel, out_shape=(pltpu.VMEM((2, 2, 128), F32), pltpu.VME...]
where the time goes in v6:
time: 28 us; the launch traced here: 27.8 us
  Pallas kernels  27.2 us (97%)
  between operations  0.64 us (2%)
    pallas_call x1, Pallas kernels, on_device(): pl.pallas_call(kernel, out_shape=(pltpu.VMEM((2, 2, 128), F32), pltpu.VME...  26.6 us
    pallas_call x1, Pallas kernels, on_device(): pl.pallas_call(finish, out_shape=results, in_specs=[vmem, vmem], out_spec...  0.6 us

profile of v6, /device:TPU:1, one launch (start us, length us, event | category | flops | bytes accessed | tf_op | source)
XLA Modules:
  0.0 27.8 jit_solution(15836179721653237369)
XLA Ops:
  0.6 26.6 %perambulator.1 = (f32[2,2,128]{2,1,0:T(2,128)S(1)}, f32[3,8]{1,0:T(4,128)S(1)}) custom-call(s32[3]{0:T(128)} %times_hbm.1, s32[3,8]{1,0:T(4,128)} %spin_hbm.1, f32[2,2,3,64,512]{4,3,2,1,0:T(8,128)} %bitcast.5, f32[2,2,24,3,4,512]{5,4,3,2,1,0:T(4,128)} %bitcast.4), custom_call_target="tpu_custom_call" | custom-call | tf_op jit(solution)/shard_map/perambulator/pallas_call | solution.py:383
  27.2 0.6 %finish.1 = (f32[2,2,128]{2,1,0:T(2,128)}, f32[3,8]{1,0:T(4,128)}) custom-call(f32[2,2,128]{2,1,0:T(2,128)S(1)} %get-tuple-element.4.block_ref, f32[3,8]{1,0:T(4,128)S(1)} %get-tuple-element.5.norm_ref), custom_call_target="tpu_custom_call" | custom-call | tf_op jit(solution)/shard_map/finish/pallas_call | solution.py:418

commit v7 on v6

--- a/solution.py
+++ b/solution.py
@@ -16,12 +16,13 @@
 SA = ("xh", "z", "core")
 COLUMN = NZ * NC
 PLANE = NXH * NY * NXL
-LATE = 13
 GUESTS = 7
 RELAY = 4
 EARLY = (0, 1, 16, 17, 2, 3, 18, 19)
 DIRECT_GUESTS = (2, 3)
 OTHERS = ((4, 16), (20, 32))
+SLOW_LO, SLOW_HI = 3, 6
+PROMPT = 16
 FAR_Y, FAR_YS, FAR_LO = 4, 2, 10
 FAR = COLUMN - FAR_LO
 DIRECT = NXH * NXL * FAR_YS * FAR
@@ -50,8 +51,7 @@
     is_guest = jnp.logical_and(first, jnp.logical_and(place >= 1, place <= GUESTS))
     is_spare = jnp.logical_and(first, place == 1)
     is_relay = jnp.logical_and(jnp.logical_not(first), place == RELAY)
-    shifted = jnp.where(place == 1, LATE, jnp.where(place <= LATE, place - 1, place))
-    me = jnp.where(jnp.logical_and(first, place >= 1), shifted, place)
+    me = place
     in_far = jnp.logical_and(y >= FAR_Y, y < FAR_Y + FAR_YS)
     is_far = jnp.logical_and(in_far, place >= FAR_LO)
     is_early = jnp.logical_or(
@@ -63,6 +63,17 @@
     for q in range(4):
         pltpu.make_async_copy(sol_hbm.at[q % 2, q // 2], sol.at[q],
                               sol_sem.at[q // 3]).start()
+    def start_eig():
+        for q in range(4):
+            pltpu.make_async_copy(eig_hbm.at[q % 2, q // 2], eig.at[q % 2, q // 2],
+                                  eig_sem).start()
+
+    eager = jnp.logical_or(y < SLOW_LO, y > SLOW_HI)
+
+    @pl.when(eager)
+    def _():
+        start_eig()
+
     int_loads = [pltpu.make_async_copy(times_hbm, times_ref, int_sem.at[0]),
                  pltpu.make_async_copy(spin_hbm, spin_ref, int_sem.at[1])]
     for copy in int_loads:
@@ -71,10 +82,6 @@
     def at_place(n):
         return {"z": n // NC, "core": 1 - lax.rem(n, NC)}
 
-    def column(o):
-        moved = jnp.where(o == LATE, 1, jnp.where(o < LATE, o + 1, o))
-        return at_place(jnp.where(jnp.logical_and(first, o >= 1), moved, o))
-
     def plane_at(d):
         return {"xh": d // (NY * NXL), "y": d // NXL % NY, "xl": d % NXL, "z": 0, "core": 1}
 
@@ -90,11 +97,13 @@
     def greet(device):
         pl.semaphore_signal(barrier, inc=1, device_id=device, device_id_type=MESH)
 
+    @pl.when(xh == 0)
+    def _():
+        greet({"xh": 1 - xh})
+
     @pl.loop(me + 1, COLUMN)
     def _(o):
-        greet(column(o))
-
-    greet({"xh": 1 - xh})
+        greet(at_place(me + COLUMN - o))
 
     @pl.when(is_root)
     def _():
@@ -117,15 +126,31 @@
                    "y": FAR_Y + lax.rem(i // FAR, FAR_YS),
                    "z": n // NC, "core": 1 - lax.rem(n, NC)})
 
-    high[...] = jnp.zeros(high.shape, BF16)
-    low[...] = jnp.zeros(low.shape, BF16)
-
-    pl.semaphore_wait(barrier, me + 1 + jnp.where(is_root, PLANE - 1 + GUESTS, 0)
-                      + jnp.where(is_far, len(EARLY) + len(DIRECT_GUESTS), 0))
-
-    @pl.loop(0, me)
-    def _(o):
-        pl.semaphore_signal(ready, inc=1, device_id=column(o), device_id_type=MESH)
+    for ref in (high, low):
+        for t in range(2):
+            for p in range(2):
+                ref[t, 128 * p + 96:128 * p + 128] = jnp.zeros((32, 1536), BF16)
+
+    def enter():
+        pl.semaphore_wait(barrier, me + xh + jnp.where(is_root, PLANE - 1 + GUESTS, 0)
+                          + jnp.where(is_far, len(EARLY) + len(DIRECT_GUESTS), 0))
+
+    def announce():
+        @pl.loop(0, me)
+        def _(o):
+            pl.semaphore_signal(ready, inc=1, device_id=at_place(o), device_id_type=MESH)
+
+        @pl.when(xh == 1)
+        def _():
+            pl.semaphore_signal(ready, inc=1, device_id={"xh": 1 - xh}, device_id_type=MESH)
+
+    prompt = jnp.logical_and(jnp.logical_not(first), place < PROMPT)
+    patient = jnp.logical_and(jnp.logical_not(first), place >= PROMPT)
+
+    @pl.when(prompt)
+    def _():
+        enter()
+        announce()
 
     squares = jnp.zeros((24, 4, 512), F32)
 
@@ -152,6 +177,10 @@
             src_ref=row, dst_ref=slot, send_sem=ssem, recv_sem=sem,
             device_id=device, device_id_type=MESH).start()
 
+    @pl.when(patient)
+    def _():
+        enter()
+
     @pl.when(is_far)
     def _():
         spot = ((xh * NXL + xl) * FAR_YS + y - FAR_Y) * FAR + place - FAR_LO
@@ -162,13 +191,17 @@
         for e in EARLY[1:]:
             send_row(rows3.at[pl.ds(spot, 1)], rsem.at[4], plane_at(e))
 
-    @pl.when(jnp.logical_not(jnp.logical_or(is_root, is_far)))
+    @pl.when(jnp.logical_not(functools.reduce(jnp.logical_or, [is_root, is_far, first])))
     def _():
         send_row(rows1.at[pl.ds(me, 1)], rsem.at[0], {"z": 0, "core": 1})
 
-    for q in range(4):
-        pltpu.make_async_copy(eig_hbm.at[q % 2, q // 2], eig.at[q % 2, q // 2],
-                              eig_sem).start()
+    @pl.when(patient)
+    def _():
+        announce()
+
+    @pl.when(jnp.logical_not(eager))
+    def _():
+        start_eig()
 
     for t in range(2):
         for p in range(2):
@@ -214,8 +247,17 @@
                 for h in range(2):
                     send[pl.ds(r * 8 + h * 4 + p * 2 + t, 8, stride=24), :] = block[8 * h:8 * h + 8]
 
+    @pl.when(first)
+    def _():
+        enter()
+
+        @pl.when(jnp.logical_not(is_root))
+        def _():
+            announce()
+            send_row(rows1.at[pl.ds(me, 1)], rsem.at[0], {"z": 0, "core": 1})
+
     def send_block(o):
-        peer = column(o)
+        peer = at_place(o)
         spot = pl.multiple_of((peer["z"] * NC + peer["core"]) * 8, 8)
         pltpu.make_async_remote_copy(
             src_ref=send.at[pl.ds(spot, 8)], dst_ref=recv.at[me],
@@ -252,9 +294,9 @@
         near[...] = jnp.sum(rows1[0:FAR_LO], axis=0, keepdims=True)
         share_early(near)
 
-    @pl.when(me < COLUMN - 1)
-    def _():
-        pl.semaphore_wait(ready, COLUMN - 1 - me)
+    @pl.when(jnp.logical_or(me < COLUMN - 1, xh == 0))
+    def _():
+        pl.semaphore_wait(ready, COLUMN - me - xh)
 
     @pl.loop(me + 1, COLUMN)
     def _(o):

time: 28 us -> 28 us (level)
  no operation moved by 1% of the time
where the time goes in v7:
time: 28 us; the launch traced here: 27.8 us
  Pallas kernels  27.2 us (97%)
  between operations  0.64 us (2%)
    pallas_call x1, Pallas kernels, on_device(): pl.pallas_call(kernel, out_shape=(pltpu.VMEM((2, 2, 128), F32), pltpu.VME...  26.6 us
    pallas_call x1, Pallas kernels, on_device(): pl.pallas_call(finish, out_shape=results, in_specs=[vmem, vmem], out_spec...  0.6 us

profile of v7, /device:TPU:1, one launch (start us, length us, event | category | flops | bytes accessed | tf_op | source)
XLA Modules:
  0.0 27.8 jit_solution(5189436406678352846)
XLA Ops:
  0.6 26.6 %perambulator.1 = (f32[2,2,128]{2,1,0:T(2,128)S(1)}, f32[3,8]{1,0:T(4,128)S(1)}) custom-call(s32[3]{0:T(128)} %times_hbm.1, s32[3,8]{1,0:T(4,128)} %spin_hbm.1, f32[2,2,3,64,512]{4,3,2,1,0:T(8,128)} %bitcast.5, f32[2,2,24,3,4,512]{5,4,3,2,1,0:T(4,128)} %bitcast.4), custom_call_target="tpu_custom_call" | custom-call | tf_op jit(solution)/shard_map/perambulator/pallas_call | solution.py:425
  27.2 0.6 %finish.1 = (f32[2,2,128]{2,1,0:T(2,128)}, f32[3,8]{1,0:T(4,128)}) custom-call(f32[2,2,128]{2,1,0:T(2,128)S(1)} %get-tuple-element.4.block_ref, f32[3,8]{1,0:T(4,128)S(1)} %get-tuple-element.5.norm_ref), custom_call_target="tpu_custom_call" | custom-call | tf_op jit(solution)/shard_map/finish/pallas_call | solution.py:460

commit v8 on v7

--- a/solution.py
+++ b/solution.py
@@ -23,6 +23,7 @@
 OTHERS = ((4, 16), (20, 32))
 SLOW_LO, SLOW_HI = 3, 6
 PROMPT = 16
+CUT = 18
 FAR_Y, FAR_YS, FAR_LO = 4, 2, 10
 FAR = COLUMN - FAR_LO
 DIRECT = NXH * NXL * FAR_YS * FAR
@@ -41,7 +42,7 @@
 def kernel(times_hbm, spin_hbm, eig_hbm, sol_hbm, out_ref, norm_ref,
            eig, sol, times_ref, spin_ref, high, low, tmp, send, recv, half, other,
            row, rows1, near, total, rows2, rows3, final, tally,
-           sol_sem, eig_sem, int_sem, ssem, rsem, ready):
+           loads, ssem, rsem, ready):
     y, xl, xh = lax.axis_index("y"), lax.axis_index("xl"), lax.axis_index("xh")
     z, core = lax.axis_index("z"), lax.axis_index("core")
     plane_me = (xh * NY + y) * NXL + xl
@@ -60,24 +61,22 @@
         jnp.logical_and(first, functools.reduce(
             jnp.logical_or, [place == n for n in DIRECT_GUESTS])))
 
-    for q in range(4):
-        pltpu.make_async_copy(sol_hbm.at[q % 2, q // 2], sol.at[q],
-                              sol_sem.at[q // 3]).start()
+    for q in range(3):
+        pltpu.make_async_copy(sol_hbm.at[q % 2, q // 2], sol.at[pl.ds(24 * q, 24)],
+                              loads.at[0]).start()
+    pltpu.make_async_copy(sol_hbm.at[1, 1, pl.ds(0, CUT)], sol.at[pl.ds(72, CUT)],
+                          loads.at[1]).start()
+    pltpu.make_async_copy(sol_hbm.at[1, 1, pl.ds(CUT, 24 - CUT)],
+                          sol.at[pl.ds(72 + CUT, 24 - CUT)], loads.at[2]).start()
+
     def start_eig():
         for q in range(4):
             pltpu.make_async_copy(eig_hbm.at[q % 2, q // 2], eig.at[q % 2, q // 2],
-                                  eig_sem).start()
+                                  loads.at[0]).start()
 
     eager = jnp.logical_or(y < SLOW_LO, y > SLOW_HI)
-
-    @pl.when(eager)
-    def _():
-        start_eig()
-
-    int_loads = [pltpu.make_async_copy(times_hbm, times_ref, int_sem.at[0]),
-                 pltpu.make_async_copy(spin_hbm, spin_ref, int_sem.at[1])]
-    for copy in int_loads:
-        copy.start()
+    int_loads = [pltpu.make_async_copy(times_hbm, times_ref, loads.at[1]),
+                 pltpu.make_async_copy(spin_hbm, spin_ref, loads.at[2])]
 
     def at_place(n):
         return {"z": n // NC, "core": 1 - lax.rem(n, NC)}
@@ -152,25 +151,37 @@
         enter()
         announce()
 
-    squares = jnp.zeros((24, 4, 512), F32)
-
     def arrived(buf, count, sem):
         pltpu.make_async_copy(buf.at[pl.ds(0, count)], buf.at[pl.ds(0, count)], sem).wait()
 
-    for q in range(4):
-        if q == 0:
-            arrived(sol, 3, sol_sem.at[0])
-        if q == 3:
-            arrived(sol, 1, sol_sem.at[1])
+    def squared(acc, start, count):
         for c in range(3):
-            piece = sol[q, :, c]
-            squares = squares + piece * piece
-
-    lanes = (squares[:, :, :128] + squares[:, :, 128:256]) + (squares[:, :, 256:384] + squares[:, :, 384:])
-    sums = jnp.sum(lanes.reshape(96, 128), axis=1, keepdims=True)
-    line = lax.broadcasted_iota(jnp.int32, (96, 128), 0)
-    spot = lax.broadcasted_iota(jnp.int32, (96, 128), 1)
-    row[...] = jnp.sum(jnp.where(line // 4 == spot, sums, F32(0)), axis=0, keepdims=True)
+            piece = sol[start:start + count, c]
+            acc = acc + piece * piece
+        return acc
+
+    def as_row(acc, start, count):
+        lanes = (acc[:, :, :128] + acc[:, :, 128:256]) + (acc[:, :, 256:384] + acc[:, :, 384:])
+        sums = jnp.sum(lanes.reshape(count * 4, 128), axis=1, keepdims=True)
+        line = lax.broadcasted_iota(jnp.int32, (count * 4, 128), 0)
+        spot = lax.broadcasted_iota(jnp.int32, (count * 4, 128), 1)
+        return jnp.sum(jnp.where(line // 4 + start == spot, sums, F32(0)), axis=0, keepdims=True)
+
+    squares = jnp.zeros((CUT, 4, 512), F32)
+    more = jnp.zeros((24 - CUT, 4, 512), F32)
+    arrived(sol, 72, loads.at[0])
+
+    @pl.when(eager)
+    def _():
+        start_eig()
+
+    for q in range(3):
+        squares = squared(squares, 24 * q, CUT)
+        more = squared(more, 24 * q + CUT, 24 - CUT)
+    arrived(sol, CUT, loads.at[1])
+    part = as_row(squared(squares, 72, CUT), 0, CUT)
+    arrived(sol, 24 - CUT, loads.at[2])
+    row[...] = part + as_row(squared(more, 72 + CUT, 24 - CUT), CUT, 24 - CUT)
 
     def send_row(slot, sem, device):
         pltpu.make_async_remote_copy(
@@ -203,16 +214,20 @@
     def _():
         start_eig()
 
+    for copy in int_loads:
+        copy.start()
+
     for t in range(2):
         for p in range(2):
             for c in range(3):
-                h, l = split(sol[2 * t + p, :, c].reshape(96, 512))
+                q = 2 * t + p
+                h, l = split(sol[24 * q:24 * q + 24, c].reshape(96, 512))
                 high[t, 128 * p:128 * p + 96, 512 * c:512 * c + 512] = h
                 low[t, 128 * p:128 * p + 96, 512 * c:512 * c + 512] = l
 
     for copy in int_loads:
         copy.wait()
-    pltpu.make_async_copy(eig, eig, eig_sem).wait()
+    pltpu.make_async_copy(eig, eig, loads.at[0]).wait()
     lane = lax.broadcasted_iota(jnp.int32, (1, 128), 1)
     lane16 = lax.broadcasted_iota(jnp.int32, (16, 128), 1)
     signs = []
@@ -348,6 +363,18 @@
             src_ref=final, dst_ref=final, send_sem=ssem, recv_sem=rsem.at[0],
             device_id=at_place(n), device_id_type=MESH)
 
+    base = 8 * (COLUMN - 1) + 4
+    plain_root = jnp.logical_and(is_root, jnp.logical_not(first))
+    first_root = jnp.logical_and(is_root, first)
+    senders = ((plain_root, PLANE - 1 + GUESTS + RELAY),
+               (is_relay, COLUMN - RELAY),
+               (is_spare, COLUMN - GUESTS))
+    others = jnp.logical_not(functools.reduce(
+        jnp.logical_or, [plain_root, is_relay, is_spare, first_root, is_far]))
+    for role, count in ((first_root, PLANE - 1 + GUESTS),
+                        (is_far, 1 + len(EARLY) + len(DIRECT_GUESTS)), (others, 1)):
+        pl.when(role)(functools.partial(arrived, tally, base + count, ssem))
+
     @pl.when(is_root)
     def _():
         arrived(tally, PLANE - 1, rsem.at[2])
@@ -370,8 +397,6 @@
     @pl.when(jnp.logical_not(summing))
     def _():
         down(0).wait_recv()
-
-    plain_root = jnp.logical_and(is_root, jnp.logical_not(first))
 
     @pl.when(plain_root)
     def _():
@@ -394,17 +419,8 @@
     for s in range(3):
         norm_ref[s:s + 1, :] = pltpu.roll(norm, (128 - 8 * s) % 128, 1)[:, :8]
 
-    base = 8 * (COLUMN - 1) + 4
-    roles = ((jnp.logical_and(is_root, first), PLANE - 1 + GUESTS),
-             (plain_root, PLANE - 1 + GUESTS + RELAY),
-             (is_relay, COLUMN - RELAY),
-             (is_spare, COLUMN - GUESTS),
-             (is_far, 1 + len(EARLY) + len(DIRECT_GUESTS)))
-    rest = True
-    for role, count in roles:
+    for role, count in senders:
         pl.when(role)(functools.partial(arrived, tally, base + count, ssem))
-        rest = jnp.logical_and(rest, jnp.logical_not(role))
-    pl.when(rest)(functools.partial(arrived, tally, base + 1, ssem))
 
 
 def finish(block_ref, norm_ref, block_out, norm_out, sem):
@@ -429,7 +445,7 @@
         out_specs=(vmem, vmem),
         scratch_shapes=[
             pltpu.VMEM((2, 2, 3, 64, 512), F32),
-            pltpu.VMEM((4, 24, 3, 4, 512), F32),
+            pltpu.VMEM((96, 3, 4, 512), F32),
             pltpu.SMEM((3,), jnp.int32),
             pltpu.SMEM((3, 8), jnp.int32),
             pltpu.VMEM((2, 256, 1536), BF16),
@@ -447,9 +463,7 @@
             pltpu.VMEM((DIRECT, 128), F32),
             pltpu.VMEM((1, 128), F32),
             pltpu.VMEM((256, 1, 128), F32),
-            pltpu.SemaphoreType.DMA((2,)),
-            pltpu.SemaphoreType.DMA,
-            pltpu.SemaphoreType.DMA((2,)),
+            pltpu.SemaphoreType.DMA((3,)),
             pltpu.SemaphoreType.DMA,
             pltpu.SemaphoreType.DMA((5,)),
             pltpu.SemaphoreType.REGULAR,

time: 28 us -> 28.1 us (level)
  no operation moved by 1% of the time
where the time goes in v8:
time: 28.1 us; the launch traced here: 27.9 us
  Pallas kernels  27.2 us (97%)
  between operations  0.64 us (2%)
    pallas_call x1, Pallas kernels, on_device(): pl.pallas_call(kernel, out_shape=(pltpu.VMEM((2, 2, 128), F32), pltpu.VME...  26.6 us
    pallas_call x1, Pallas kernels, on_device(): pl.pallas_call(finish, out_shape=results, in_specs=[vmem, vmem], out_spec...  0.6 us

profile of v8, /device:TPU:1, one launch (start us, length us, event | category | flops | bytes accessed | tf_op | source)
XLA Modules:
  0.0 27.9 jit_solution(8031636331841976626)
XLA Ops:
  0.6 26.6 %perambulator.1 = (f32[2,2,128]{2,1,0:T(2,128)S(1)}, f32[3,8]{1,0:T(4,128)S(1)}) custom-call(s32[3]{0:T(128)} %times_hbm.1, s32[3,8]{1,0:T(4,128)} %spin_hbm.1, f32[2,2,3,64,512]{4,3,2,1,0:T(8,128)} %bitcast.5, f32[2,2,24,3,4,512]{5,4,3,2,1,0:T(4,128)} %bitcast.4), custom_call_target="tpu_custom_call" | custom-call | tf_op jit(solution)/shard_map/perambulator/pallas_call | solution.py:441
  27.3 0.6 %finish.1 = (f32[2,2,128]{2,1,0:T(2,128)}, f32[3,8]{1,0:T(4,128)}) custom-call(f32[2,2,128]{2,1,0:T(2,128)S(1)} %get-tuple-element.4.block_ref, f32[3,8]{1,0:T(4,128)S(1)} %get-tuple-element.5.norm_ref), custom_call_target="tpu_custom_call" | custom-call | tf_op jit(solution)/shard_map/finish/pallas_call | solution.py:474

commit v9 on v7

--- a/solution.py
+++ b/solution.py
@@ -23,7 +23,7 @@
 OTHERS = ((4, 16), (20, 32))
 SLOW_LO, SLOW_HI = 3, 6
 PROMPT = 16
-FAR_Y, FAR_YS, FAR_LO = 4, 2, 10
+FAR_Y, FAR_YS, FAR_LO = 4, 2, 12
 FAR = COLUMN - FAR_LO
 DIRECT = NXH * NXL * FAR_YS * FAR
 

time: 28 us -> 28 us (level)
  no operation moved by 1% of the time
where the time goes in v9:
time: 28 us; the launch traced here: 27.8 us
  Pallas kernels  27.2 us (97%)
  between operations  0.64 us (2%)
    pallas_call x1, Pallas kernels, on_device(): pl.pallas_call(kernel, out_shape=(pltpu.VMEM((2, 2, 128), F32), pltpu.VME...  26.6 us
    pallas_call x1, Pallas kernels, on_device(): pl.pallas_call(finish, out_shape=results, in_specs=[vmem, vmem], out_spec...  0.6 us

profile of v9, /device:TPU:1, one launch (start us, length us, event | category | flops | bytes accessed | tf_op | source)
XLA Modules:
  0.0 27.8 jit_solution(8311861494561394478)
XLA Ops:
  0.6 26.6 %perambulator.1 = (f32[2,2,128]{2,1,0:T(2,128)S(1)}, f32[3,8]{1,0:T(4,128)S(1)}) custom-call(s32[3]{0:T(128)} %times_hbm.1, s32[3,8]{1,0:T(4,128)} %spin_hbm.1, f32[2,2,3,64,512]{4,3,2,1,0:T(8,128)} %bitcast.5, f32[2,2,24,3,4,512]{5,4,3,2,1,0:T(4,128)} %bitcast.4), custom_call_target="tpu_custom_call" | custom-call | tf_op jit(solution)/shard_map/perambulator/pallas_call | solution.py:425
  27.2 0.6 %finish.1 = (f32[2,2,128]{2,1,0:T(2,128)}, f32[3,8]{1,0:T(4,128)}) custom-call(f32[2,2,128]{2,1,0:T(2,128)S(1)} %get-tuple-element.4.block_ref, f32[3,8]{1,0:T(4,128)S(1)} %get-tuple-element.5.norm_ref), custom_call_target="tpu_custom_call" | custom-call | tf_op jit(solution)/shard_map/finish/pallas_call | solution.py:460
